TPU v7x, 256 devices: a whole 4x4x8 slice. The times are simulated.
256 devices in a mesh: cfg: 2 (over y_hi), seq: 16 (over z, core), tp: 8 (over y_lo, x).
Axes of the slice: x: 4, y: 4 (y_hi: 2, y_lo: 2; y = y_hi * 2 + y_lo), z: 8, core: 2. Of those that a mesh axis runs over, the one named last changes fastest.
Arguments:
- queries: bfloat16 [2, 7680, 5120], P('cfg', 'seq', 'tp'), may hold values from -5 to 5
- keys: bfloat16 [2, 7680, 5120], P('cfg', 'seq', 'tp'), may hold values from -5 to 5
- values: bfloat16 [2, 7680, 5120], P('cfg', 'seq', 'tp'), may hold values from -5 to 5
- text_keys: bfloat16 [2, 512, 5120], P('cfg', None, 'tp'), may hold values from -7.5 to 7.5
- text_values: bfloat16 [2, 512, 5120], P('cfg', None, 'tp'), may hold values from -5 to 5
- prompt_lengths: int32 [2], P('cfg'), may hold values from 64 to 512
- frame_counts: int32 [16], P('seq'), may hold values from 240 to 480
- out_weight: bfloat16 [5120, 5120], P('tp'), may hold values from -0.5 to 0.5
Outputs:
- velocity: bfloat16 [7680, 5120], P('seq', ('tp', 'cfg'))
All inputs are finite; a program needn't handle non-finite values.
Results may differ from a plain program's by a relative error of at most 0.015.
Values may be sent and summed in bfloat16 or wider, within the bound.
A program may use at most 256 MiB of HBM per device.

v0:
```python
import jax
import jax.numpy as jnp
from jax import lax
from jax.sharding import PartitionSpec as P

HEAD_DIM = 128
FRAME_SLOTS = 480


GUIDANCE = 5.0
RESCALE = 0.7
NEGATIVE = -1e30


def in_order(pieces, dim):
    dims = list(pieces.shape[1:])
    dims[dim] *= pieces.shape[0]
    return jnp.moveaxis(pieces, 0, dim).reshape(dims)


def from_everyone(value, axis):
    devices = lax.axis_size(axis)
    return lax.all_to_all(
        jnp.broadcast_to(value[None], (devices, *value.shape)), axis, 0, 0, tiled=True
    )


def gathered_copies(value, axis, dim):
    return in_order(from_everyone(value, axis), dim)


def of_everyone(value, axis):
    return from_everyone(value, axis).sum(axis=0)


def together(arrays, axis):
    ends = [0]
    for a in arrays:
        ends.append(ends[-1] + a.size)
    running = of_everyone(jnp.concatenate([a.ravel() for a in arrays]), axis)
    return tuple((running[b:e].reshape(a.shape) for a, b, e in zip(arrays, ends, ends[1:])))


def frame_valid(positions, counts_table):
    frame_index = positions // FRAME_SLOTS
    slot_index = positions % FRAME_SLOTS
    frame_ids = jnp.arange(counts_table.shape[0], dtype=jnp.int32)
    frame_limit = jnp.sum(
        jnp.where(frame_index[:, None] == frame_ids[None, :], counts_table[None, :], 0), axis=1
    )
    return slot_index < frame_limit


def attend_block(carry, key_rows, value_rows, query_heads, key_mask):
    row_max, weight_sum, mixed_sum = carry
    head_count = query_heads.shape[1]
    key_heads = key_rows.reshape(key_rows.shape[0], head_count, HEAD_DIM)
    value_heads = value_rows.reshape(value_rows.shape[0], head_count, HEAD_DIM)
    scores = jnp.einsum(
        "qhd,khd->hqk", query_heads, key_heads, preferred_element_type=jnp.float32
    ) * HEAD_DIM ** (-0.5)
    scores = jnp.where(key_mask[None, None, :], scores, NEGATIVE)
    new_max = jnp.maximum(row_max, jnp.max(scores, axis=2))
    shrink = jnp.exp(row_max - new_max)
    weights = jnp.exp(scores - new_max[:, :, None])
    weight_sum = weight_sum * shrink + jnp.sum(weights, axis=2)
    mixed_sum = mixed_sum * shrink[:, :, None] + jnp.einsum(
        "hqk,khd->hqd",
        weights.astype(jnp.bfloat16),
        value_heads,
        preferred_element_type=jnp.float32,
    )
    return (new_max, weight_sum, mixed_sum)


def body(queries, keys, values, text_keys, text_values, prompt_lengths, frame_counts, out_weight):
    row_count = queries.shape[1]
    head_cols = queries.shape[2]
    head_count = head_cols // HEAD_DIM
    all_counts = gathered_copies(frame_counts, "seq", 0)
    query_heads = queries[0].reshape(row_count, head_count, HEAD_DIM)
    text_mask = jnp.arange(text_keys.shape[1], dtype=jnp.int32) < prompt_lengths[0]
    empty_state = (
        jnp.full((head_count, row_count), NEGATIVE, jnp.float32),
        jnp.zeros((head_count, row_count), jnp.float32),
        jnp.zeros((head_count, row_count, HEAD_DIM), jnp.float32),
    )
    text_state = attend_block(empty_state, text_keys[0], text_values[0], query_heads, text_mask)
    key_rows = lax.all_gather(keys[0], "seq", axis=0, tiled=True)
    value_rows = lax.all_gather(values[0], "seq", axis=0, tiled=True)
    positions = jnp.arange(key_rows.shape[0], dtype=jnp.int32)
    row_max, weight_sum, mixed_sum = attend_block(
        text_state, key_rows, value_rows, query_heads, frame_valid(positions, all_counts)
    )
    attended = (
        jnp.transpose(mixed_sum / weight_sum[:, :, None], (1, 0, 2))
        .reshape(row_count, head_cols)
        .astype(jnp.bfloat16)
    )
    projected = (
        lax.psum_scatter(
            lax.dot_general(
                out_weight, attended, (((0,), (1,)), ((), ())), preferred_element_type=jnp.float32
            ).astype(jnp.bfloat16),
            "tp",
            scatter_dimension=0,
            tiled=True,
        )
        .astype(jnp.float32)
        .T
    )
    branch = projected.astype(jnp.bfloat16)[None]
    paired = lax.all_to_all(branch, "cfg", split_axis=2, concat_axis=0, tiled=True)
    conditional = paired[0].astype(jnp.float32)
    unconditional = paired[1].astype(jnp.float32)
    guided = unconditional + GUIDANCE * (conditional - unconditional)
    token_weights = frame_valid(jnp.arange(row_count, dtype=jnp.int32), frame_counts).astype(
        jnp.float32
    )

    def local_sum(field_rows):
        return jnp.dot(token_weights, field_rows)

    guided_sum, guided_square, cond_sum, cond_square = together(
        (
            local_sum(guided),
            local_sum(guided * guided),
            local_sum(conditional),
            local_sum(conditional * conditional),
        ),
        "seq",
    )
    valid_total = jnp.sum(all_counts).astype(jnp.float32)
    guided_mean = guided_sum / valid_total
    guided_var = guided_square / valid_total - guided_mean * guided_mean
    cond_mean = cond_sum / valid_total
    cond_var = cond_square / valid_total - cond_mean * cond_mean
    std_ratio = jnp.sqrt((cond_var + 1.0) / (guided_var + 1.0))
    factor = RESCALE * std_ratio + (1.0 - RESCALE)
    return (guided_mean + (guided - guided_mean) * factor).astype(jnp.bfloat16)


def solution(mesh):
    placed = (
        P("cfg", "seq", "tp"),
        P("cfg", "seq", "tp"),
        P("cfg", "seq", "tp"),
        P("cfg", None, "tp"),
        P("cfg", None, "tp"),
        P("cfg"),
        P("seq"),
        P("tp", None),
    )
    return jax.shard_map(
        body, mesh=mesh, in_specs=placed, out_specs=P("seq", ("tp", "cfg")), check_vma=False
    )
```

profile of v0, /device:TPU:1, one launch (start us, length us, event | category | flops | bytes accessed | tf_op | source)
XLA Modules:
  0.0 327.0 jit_solution(5678599585954011462)
XLA Ops:
  6.5 0.0 all-gather.5.cloned.1.call-start
  6.5 0.7 all-gather.5.cloned.1.call-update
  7.3 0.0 all-gather.7.cloned.1.call-start
  7.3 0.7 all-gather.7.cloned.1.call-update
  8.7 0.6 broadcast_in_dim.95
  9.3 10.0 %all-to-all-start = ((s32[16,1,1]{2,1,0:T(1,128)}), s32[16,1,1]{2,1,0:T(1,128)S(1)}, u32[]{:S(2)}, u32[]{:S(2)}) async-start(s32[16,1,1]{2,1,0:T(1,128)} %broadcast_in_dim.95), calls=%async_computation | async-start | bytes 16384 | tf_op jit(solution)/shard_map/all_to_all | solution.py:23
  19.2 0.0 reduce-scatter.4.cloned.1.call-start
  19.3 1.3 copy.70
  21.2 1.3 copy.71
  22.6 3.2 fusion.7
  25.9 0.2 copy.74
  26.1 0.1 all-to-all-done
  26.2 1.0 fusion.62
  27.2 0.2 select_reduce_fusion
  27.4 48.6 %all-gather.5.cloned.1.call-done = bf16[1,7680,640]{2,1,0:T(8,128)(2,1)} async-done(((bf16[1,480,640]{2,1,0:T(8,128)(2,1)}), bf16[1,7680,640]{2,1,0:T(8,128)(2,1)}) %all-gather.5.cloned.1.call-update) | async-done | bytes 9830416 | tf_op jit(solution)/shard_map/all_gather | solution.py:89
  76.0 13.7 %copy.76 = bf16[1,7680,640]{1,2,0:T(8,128)(2,1)} copy(bf16[1,7680,640]{2,1,0:T(8,128)(2,1)} %all-gather.5.cloned.1.call-done) | data formatting | bytes 19660800 | tf_op jit(solution)/shard_map/all_gather | solution.py:89
  89.8 31.7 %fusion = (f32[5,480]{1,0:T(8,128)S(1)}, f32[5,480,7680]{2,1,0:T(8,128)}) fusion(pred[7680]{0:T(1024)(128)(4,1)S(1)} %fusion.41, bf16[480,5,128]{0,2,1:T(8,128)(2,1)S(1)} %bitcast.102, bf16[7680,5,128]{0,2,1:T(8,128)(2,1)} %bitcast.97), kind=kOutput, calls=%fused_computation.2 | convolution fusion | flops 4773885440 | bytes 84190080 | tf_op jit(solution)/shard_map/qhd,khd->hqk/dot_general | solution.py:59
  121.5 3.9 %fusion.8 = f32[5,480]{1,0:T(8,128)S(1)} fusion(f32[5,480,512]{2,1,0:T(8,128)} %get-tuple-element.17, f32[5,480]{1,0:T(8,128)S(1)} %get-tuple-element.11, pred[512]{0:T(512)(128)(4,1)S(1)} %iota_compare_fusion.2), kind=kLoop, calls=%fused_computation.12 | loop fusion | flops 4912800 | bytes 4934912 | tf_op jit(solution)/shard_map/reduce_sum | solution.py:66
  125.4 23.8 %fusion.1 = f32[5,480]{1,0:T(8,128)S(1)} fusion(f32[5,480,7680]{2,1,0:T(8,128)} %get-tuple-element.15, f32[5,480]{1,0:T(8,128)S(1)} %get-tuple-element.10, pred[7680]{0:T(1024)(128)(4,1)S(1)} %fusion.41), kind=kLoop, calls=%fused_computation.3 | loop fusion | flops 73725600 | bytes 73754880 | tf_op jit(solution)/shard_map/reduce_sum | solution.py:66
  149.3 1.7 fusion.28
  150.9 0.0 all-gather.7.cloned.1.call-done
  151.0 13.7 %copy.79 = bf16[1,7680,640]{1,2,0:T(8,128)(2,1)} copy(bf16[1,7680,640]{2,1,0:T(8,128)(2,1)} %all-gather.7.cloned.1.call-done) | data formatting | bytes 19660800 | tf_op jit(solution)/shard_map/all_gather | solution.py:90
  164.7 29.4 %fusion.34 = bf16[480,5,128]{2,0,1:T(8,128)(2,1)S(1)} fusion(f32[480,5,128]{2,0,1:T(8,128)S(1)} %fusion.28, bf16[7680,5,128]{0,2,1:T(8,128)(2,1)} %bitcast.100, f32[5,480,7680]{2,1,0:T(8,128)} %get-tuple-element.15, f32[5,480]{1,0:T(8,128)S(1)} %get-tuple-element.10, pred[7680]{0:T(1024)(128)(4,1)S(1)} %fusion.41, f32[480,5]{0,1:T(8,128)S(1)} %get-tuple-element.7), kind=kOutput, calls=%fused_computation.25 | convolution fusion | flops 4793241600 | bytes 85428480 | tf_op jit(solution)/shard_map/hqk,khd->hqd/dot_general | solution.py:67
  194.1 0.2 copy.81
  194.3 8.8 %fusion.6 = bf16[5120,480]{0,1:T(8,128)(2,1)} fusion(bf16[480,640]{0,1:T(8,128)(2,1)S(1)} %bitcast.116, bf16[640,5120]{1,0:T(8,128)(2,1)} %param.15), kind=kOutput, calls=%fused_computation.8 | convolution fusion | flops 3148185600 | bytes 12083200 | tf_op jit(solution)/shard_map/dot_general | solution.py:102
  203.2 7.8 %copy.91 = bf16[5120,480]{1,0:T(8,128)(2,1)} copy(bf16[5120,480]{0,1:T(8,128)(2,1)} %fusion.6) | data formatting | bytes 9830400
  211.0 0.0 reduce-scatter.4.cloned.1.call-update
  211.0 64.1 %reduce-scatter.4.cloned.1.call-done = bf16[640,480]{1,0:T(8,128)(2,1)} async-done(((bf16[5120,480]{1,0:T(8,128)(2,1)}), bf16[640,480]{1,0:T(8,128)(2,1)}) %reduce-scatter.4.cloned.1.call-update) | async-done | bytes 614416
  275.1 1.4 copy.92
  276.5 1.9 copy.82
  278.4 0.5 broadcast.122
  278.9 4.8 %reduce.13 = bf16[640,480]{1,0:T(8,128)(2,1)S(1)} reduce(bf16[640,1,480]{2,1,0:T(2,128)(2,1)S(1)} %bitcast.103, bf16[]{:T(256)} %broadcast.122), dimensions={1}, to_apply=%bitcast.78.reduce_sub_computation | reduce | bytes 1228802
  283.7 2.2 reshape.116
  285.9 3.7 %all-to-all-start.1 = ((bf16[2,2,76800]{2,1,0:T(2,128)(2,1)}), bf16[2,2,76800]{2,1,0:T(2,128)(2,1)S(1)}, u32[]{:S(2)}, u32[]{:S(2)}) async-start(bf16[2,2,76800]{2,1,0:T(2,128)(2,1)} %reshape.116), calls=%async_computation.1 | async-start | bytes 1228800 | tf_op jit(solution)/shard_map/all_to_all | solution.py:113
  289.7 9.5 %all-to-all-done.1 = bf16[2,2,76800]{2,1,0:T(2,128)(2,1)S(1)} async-done(((bf16[2,2,76800]{2,1,0:T(2,128)(2,1)}), bf16[2,2,76800]{2,1,0:T(2,128)(2,1)S(1)}, u32[]{:S(2)}, u32[]{:S(2)}) %all-to-all-start.1) | async-done | bytes 614432 | tf_op jit(solution)/shard_map/all_to_all | solution.py:113
  299.2 1.3 reshape.117
  300.5 0.2 copy.93
  300.6 0.2 convolution_reduce_fusion
  300.9 0.2 convolution_reduce_fusion.3
  301.1 0.3 convolution_reduce_fusion.1
  301.3 0.3 convolution_reduce_fusion.2
  301.6 0.1 concatenate.3
  301.7 0.7 broadcast_in_dim.102
  302.4 8.9 %all-to-all-start.2 = ((f32[16,1,1280]{2,1,0:T(1,128)}), f32[16,1,1280]{2,1,0:T(1,128)S(1)}, u32[]{:S(2)}, u32[]{:S(2)}) async-start(f32[16,1,1280]{2,1,0:T(1,128)} %broadcast_in_dim.102), calls=%async_computation.2 | async-start | bytes 163840 | tf_op jit(solution)/shard_map/all_to_all | solution.py:23
  311.9 7.5 %all-to-all-done.2 = f32[16,1,1280]{2,1,0:T(1,128)S(1)} async-done(((f32[16,1,1280]{2,1,0:T(1,128)}), f32[16,1,1280]{2,1,0:T(1,128)S(1)}, u32[]{:S(2)}, u32[]{:S(2)}) %all-to-all-start.2) | async-done | bytes 81952 | tf_op jit(solution)/shard_map/all_to_all | solution.py:23
  319.4 0.1 reduce_sum.58
  319.4 0.1 slice_divide_fusion
  319.5 0.9 add_convert_fusion
  (14 shorter events, 0.1 us)
Async XLA Ops:
  6.5 19.3 %copy-start = (bf16[1,512,640]{2,1,0:T(8,128)(2,1)S(1)}, bf16[1,512,640]{2,1,0:T(8,128)(2,1)}, u32[]{:S(2)}) copy-start(bf16[1,512,640]{2,1,0:T(8,128)(2,1)} %param.12) | copy-start | bytes 1966084
  6.5 69.5 %all-gather.5.cloned.1.call-start = ((), (), s32[]{:S(2)}) async-start(), calls=%async_computation.4 | async-start | bytes 10444800 | tf_op jit(solution)/shard_map/all_gather | solution.py:89
  7.3 143.7 %all-gather.7.cloned.1.call-start = ((), (), s32[]{:S(2)}) async-start(), calls=%async_computation.5 | async-start | bytes 10444800 | tf_op jit(solution)/shard_map/all_gather | solution.py:90
  9.3 16.9 %all-to-all-start = ((s32[16,1,1]{2,1,0:T(1,128)}), s32[16,1,1]{2,1,0:T(1,128)S(1)}, u32[]{:S(2)}, u32[]{:S(2)}) async-start(s32[16,1,1]{2,1,0:T(1,128)} %broadcast_in_dim.95), calls=%async_computation | async-start | bytes 16384 | tf_op jit(solution)/shard_map/all_to_all | solution.py:23
  19.2 255.8 %reduce-scatter.4.cloned.1.call-start = ((), (), s32[]{:S(2)}) async-start(), calls=%async_computation.6 | async-start | bytes 5898240
  121.5 27.8 %slice-start = ((s8[4915200]{0:T(1024)(128)(4,1)}), s8[4194304]{0:T(1024)(128)(4,1)S(1)}, s32[]{:S(2)}) async-start(s8[4915200]{0:T(1024)(128)(4,1)} %bitcast.98), calls=%async_computation.7 | async-start | bytes 8388608
  125.4 23.9 %slice-start.1 = ((s8[4915200]{0:T(1024)(128)(4,1)}), s8[720896]{0:T(1024)(128)(4,1)S(1)}, s32[]{:S(2)}) async-start(s8[4915200]{0:T(1024)(128)(4,1)} %bitcast.98), calls=%async_computation.8 | async-start | bytes 1441792
  285.9 13.3 %all-to-all-start.1 = ((bf16[2,2,76800]{2,1,0:T(2,128)(2,1)}), bf16[2,2,76800]{2,1,0:T(2,128)(2,1)S(1)}, u32[]{:S(2)}, u32[]{:S(2)}) async-start(bf16[2,2,76800]{2,1,0:T(2,128)(2,1)} %reshape.116), calls=%async_computation.1 | async-start | bytes 1228800 | tf_op jit(solution)/shard_map/all_to_all | solution.py:113
  302.4 17.0 %all-to-all-start.2 = ((f32[16,1,1280]{2,1,0:T(1,128)}), f32[16,1,1280]{2,1,0:T(1,128)S(1)}, u32[]{:S(2)}, u32[]{:S(2)}) async-start(f32[16,1,1280]{2,1,0:T(1,128)} %broadcast_in_dim.102), calls=%async_computation.2 | async-start | bytes 163840 | tf_op jit(solution)/shard_map/all_to_all | solution.py:23
Sparse Core Ops, SparseCore 0:
  9.2 66.8 all-gather.4
  77.9 61.1 all-gather.6
  211.1 63.8 reduce-scatter.3
where the time goes:
time: 328 us; the launch traced here: 327 us
  waiting for transfers between devices  131 us (40%)
  matrix products  75.7 us (23%)
  local copies, waits for them, and re-layouts  47.3 us (14%)
  other arithmetic  34.9 us (11%)
  starting transfers between devices  22.6 us (7%)
  between operations  15.2 us (5%)
    unnamed x4, waiting for transfers between devices  65.5 us
    all_gather x1, waiting for transfers between devices, body(): key_rows = lax.all_gather(keys[0], 'seq', axis=0, tiled=True)  48.6 us
    dot_general x2, matrix products, attend_block(): jnp.einsum('qhd,khd->hqk', query_heads, key_heads, preferred_element_type...  34.9 us
    dot_general x2, matrix products, attend_block(): jnp.einsum('hqk,khd->hqd', weights.astype(jnp.bfloat16), value_heads, pre...  31 us
    reduce_sum x2, other arithmetic, attend_block(): weight_sum = weight_sum * shrink + jnp.sum(weights, axis=2)  27.8 us
    all_to_all x2, starting transfers between devices, from_everyone(): lax.all_to_all(jnp.broadcast_to(value[None], (devices, *value.shape)), ax...  18.8 us
    unnamed x15, local copies, waits for them, and re-layouts  16.3 us
    all_gather x1, local copies, waits for them, and re-layouts, body(): value_rows = lax.all_gather(values[0], 'seq', axis=0, tiled=True)  13.7 us
  transfers between devices with their start and end apart: 6, of which 5 were waited for; matrix products, arithmetic and copies ran while one was open for 25% of the time, Pallas kernels for 0%

commit v1 on v0

v1 whole, which is shorter than its diff:
```python
import functools

import jax
import jax.numpy as jnp
from jax import lax
from jax.experimental import pallas as pl
from jax.experimental.pallas import tpu as pltpu
from jax.sharding import PartitionSpec as P

MESH = pl.DeviceIdType.MESH
HD = 128
GUIDANCE = 5.0
RESCALE = 0.7
NEGATIVE = -1e30
LOG2E = 1.4426950408889634
F32 = jnp.float32
BF16 = jnp.bfloat16


def kernel(
    dims,
    plen_ref, count_ref, cnt_in, q_ref, k_ref, v_ref, tk_ref, tv_ref, w_hbm,
    out_ref,
    kbuf, vbuf, valid, tkbuf, tvbuf, tvalid, cbuf, m_ref, acc, obuf, wbuf,
    oacc, mine, give, got, stat, statbuf,
    ring_send, ring_recv, d2d_send, d2d_recv, cnt_send, cnt_recv,
    o_send, o_recv, w_send, w_recv, wd_send, wd_recv, w_loc,
    x_send, x_recv, st_send, st_recv,
):
    heads, rows, trows, nseq, ntp, cols = dims
    nz = nseq // 2
    half = rows // 2
    wide = out_ref.shape[1] + 64
    scale = HD ** (-0.5) * LOG2E
    me = lax.axis_index("seq")
    tp = lax.axis_index("tp")
    cfg = lax.axis_index("cfg")
    z = me // 2
    core = lax.rem(me, 2)
    up = lax.rem(z + 1, nz) * 2 + core
    down = lax.rem(z + nz - 1, nz) * 2 + core
    mate = z * 2 + (1 - core)
    count = count_ref[0]
    plen = plen_ref[0]

    def remote(src, dst, ss, rs, **to):
        return pltpu.make_async_remote_copy(
            src_ref=src, dst_ref=dst, send_sem=ss, recv_sem=rs,
            device_id=to, device_id_type=MESH,
        )

    row_id = lax.broadcasted_iota(jnp.int32, (rows, HD), 0)
    trow_id = lax.broadcasted_iota(jnp.int32, (trows, HD), 0)
    for h in range(heads):
        cut = slice(h * HD, (h + 1) * HD)
        kk = k_ref[:, cut].astype(F32)
        vv = v_ref[:, cut].astype(F32)
        kbuf[h, 0:rows, :] = jnp.where(row_id < count, kk, kk[0:1, :]).astype(BF16)
        vbuf[h, 0:rows, :] = jnp.where(row_id < count, vv, 0.0).astype(BF16)

    barrier = pltpu.get_barrier_semaphore()
    for d in range(1, nseq):
        pl.semaphore_signal(barrier, inc=1, device_id={"seq": lax.rem(me + d, nseq)}, device_id_type=MESH)
    for d in range(1, ntp):
        pl.semaphore_signal(barrier, inc=1, device_id={"tp": lax.rem(tp + d, ntp)}, device_id_type=MESH)
    pl.semaphore_signal(barrier, inc=1, device_id={"cfg": 1 - cfg}, device_id_type=MESH)
    pl.semaphore_wait(barrier, nseq - 1 + ntp - 1 + 1)

    def slot(kind, s):
        if s == 4:
            return 14
        return 2 + 4 * (s - 1) + (0 if kind < 2 else 2)

    def buf_of(kind):
        return kbuf if kind % 2 == 0 else vbuf

    def at(kind, h, sl):
        return buf_of(kind).at[h, pl.ds(sl * rows, rows), :]

    def last(kind):
        return 4 if kind in (0, 3) else 3

    def ring(h, kind, s):
        src = at(kind, h, 0 if s == 1 else slot(kind, s - 1))
        return remote(src, at(kind, h, slot(kind, s)), ring_send.at[h, kind, s - 1],
                      ring_recv.at[h, kind, s - 1], seq=(up if kind < 2 else down))

    def d2d_index(kind, s):
        if s == 0:
            return 0
        if s == 4:
            return 7
        return s if kind < 2 else 3 + s

    def d2d(h, kind, s):
        sl = 0 if s == 0 else slot(kind, s)
        i = d2d_index(kind, s)
        return remote(at(kind, h, sl), at(kind, h, sl + 1), d2d_send.at[h, kind % 2, i],
                      d2d_recv.at[h, kind % 2, i], seq=mate)

    def launch(h):
        for kind in (0, 2, 1, 3):
            ring(h, kind, 1).start()
        d2d(h, 0, 0).start()
        d2d(h, 1, 0).start()

    def pass_on(h, kind, s):
        if s > last(kind):
            return
        ring(h, kind, s).wait_recv()
        if s < last(kind):
            ring(h, kind, s + 1).start()
        d2d(h, kind, s).start()

    def cnt(d):
        peer = lax.rem(me + d, nseq)
        return remote(cnt_in, cbuf.at[me], cnt_send.at[d], cnt_recv.at[d], seq=peer)

    def wcopy(d):
        peer = lax.rem(tp + d, ntp)
        return remote(
            w_hbm.at[:, pl.ds(core * 64, 64), pl.ds(pl.multiple_of(peer * cols, HD), cols)],
            wbuf.at[:, pl.ds(tp * HD + core * 64, 64), :],
            w_send.at[d], w_recv.at[d], tp=peer)

    def wmate(d):
        src = lax.rem(tp + ntp - d, ntp)
        part = wbuf.at[:, pl.ds(src * HD + core * 64, 64), :]
        return remote(part, part, wd_send.at[d], wd_recv.at[d], seq=mate)

    def ocopy(h, d):
        peer = lax.rem(tp + d, ntp)
        return remote(obuf.at[h, tp], obuf.at[h, tp], o_send.at[h, d], o_recv.at[h, d], tp=peer)

    for d in range(1, nseq):
        cnt(d).start()
    launch(0)
    own_w = pltpu.make_async_copy(
        w_hbm.at[:, :, pl.ds(pl.multiple_of(tp * cols, HD), cols)],
        wbuf.at[:, pl.ds(tp * HD, HD), :], w_loc)
    own_w.start()
    for d in range(1, ntp):
        wcopy(d).start()

    for h in range(heads):
        cut = slice(h * HD, (h + 1) * HD)
        kk = tk_ref[:, cut].astype(F32)
        vv = tv_ref[:, cut].astype(F32)
        tkbuf[h] = jnp.where(trow_id < plen, kk, kk[0:1, :]).astype(BF16)
        tvbuf[h] = jnp.where(trow_id < plen, vv, 0.0).astype(BF16)
    tvalid[...] = jnp.where(trow_id < plen, 1.0, 0.0).astype(BF16)

    cbuf[me] = jnp.broadcast_to(count.astype(F32), cbuf.shape[1:])
    for d in range(1, nseq):
        cnt(d).wait_recv()
    for sl in range(nseq):
        if sl < 2:
            zz, other = z, sl
        elif sl >= 14:
            zz, other = lax.rem(z + 4, nz), sl - 14
        else:
            s, r = 1 + (sl - 2) // 4, (sl - 2) % 4
            zz = lax.rem(z + nz - s, nz) if r < 2 else lax.rem(z + s, nz)
            other = r % 2
        src = zz * 2 + (core if other == 0 else 1 - core)
        c = cbuf[src][0:1, :]
        valid[sl * rows:(sl + 1) * rows, :] = jnp.where(row_id.astype(F32) < c, 1.0, 0.0).astype(BF16)

    def spread(x, n):
        full, rest = divmod(n, HD)
        parts = [x] * full + ([x[:, :rest]] if rest else [])
        return parts[0] if len(parts) == 1 else jnp.concatenate(parts, axis=1)

    def attend(h, part, k, v, ok, first=False):
        r = pl.ds(part * half, half)
        q = q_ref[r, pl.ds(pl.multiple_of(h * HD, HD), HD)]
        s = lax.dot_general(q, k, (((1,), (1,)), ((), ())), preferred_element_type=F32)
        n = s.shape[1]
        mb = jnp.max(s, axis=1, keepdims=True) * scale
        if first:
            m_new = jnp.broadcast_to(mb, (half, HD))
        else:
            m_old = m_ref[r, :]
            m_new = jnp.maximum(m_old, mb)
        p = jnp.exp2(s * scale - spread(m_new, n)).astype(BF16)
        pv = lax.dot_general(p, jnp.concatenate([v, ok], axis=1), (((1,), (0,)), ((), ())),
                             preferred_element_type=F32)
        if first:
            acc[r, :] = pv
        else:
            shrink = jnp.exp2(m_old - m_new)
            acc[r, :] = acc[r, :] * jnp.concatenate([shrink, shrink], axis=1) + pv
        m_ref[r, :] = m_new

    def attend_slots(h, part, sl, n):
        r = pl.ds(sl * rows, n * rows)
        attend(h, part, kbuf[h, r, :], vbuf[h, r, :], valid[r, :])

    def project(h, first=False):
        lhs = jnp.concatenate([obuf[h, j] for j in range(ntp)], axis=1)
        res = jnp.dot(lhs, wbuf[h], preferred_element_type=F32)
        if first:
            oacc[...] = res
        else:
            oacc[...] += res

    oacc[...] = jnp.zeros_like(oacc)

    def head_step(h, _):
        for part in range(2):
            attend(h, part, tkbuf[h], tvbuf[h], tvalid[...], first=True)

        @pl.when(h == 2)
        def _():
            for d in range(1, ntp):
                wcopy(d).wait_recv()
                wmate(d).start()

        for s in range(1, 5):
            pass_on(h, 0, s)
            pass_on(h, 2, s)
            if s == 1:
                d2d(h, 0, 0).wait_recv()
                d2d(h, 1, 0).wait_recv()
                attend_slots(h, 0, 0, 2)
            else:
                for kind in range(4):
                    d2d(h, kind, s - 1).wait_recv()
                attend_slots(h, 0, 2 + 4 * (s - 2), 4)
            pass_on(h, 1, s)
            pass_on(h, 3, s)
            if s == 3:
                @pl.when(h < heads - 1)
                def _():
                    launch(h + 1)
            if s == 1:
                attend_slots(h, 1, 0, 2)
            else:
                attend_slots(h, 1, 2 + 4 * (s - 2), 4)
            if s == 3:
                @pl.when(h == 2)
                def _():
                    own_w.wait()
                    for d in range(1, ntp):
                        wmate(d).wait_recv()

                @pl.when(h >= 2)
                def _():
                    for d in range(1, ntp):
                        ocopy(h - 2, d).wait_recv()
                    project(h - 2)
        d2d(h, 0, 4).wait_recv()
        d2d(h, 3, 4).wait_recv()
        for part in range(2):
            attend_slots(h, part, 14, 2)
            r = pl.ds(part * half, half)
            obuf[h, tp, r, :] = (acc[r, 0:HD] / acc[r, HD:2 * HD]).astype(BF16)
        for d in range(1, ntp):
            ocopy(h, d).start()
        return 0

    lax.fori_loop(0, heads, head_step, 0)

    for h in (heads - 2, heads - 1):
        for d in range(1, ntp):
            ocopy(h, d).wait_recv()
        project(h)

    out = oacc[...]
    low, high = out[:, 0:wide], out[:, cols - wide:]
    mine[...] = jnp.where(cfg == 0, low, high).astype(BF16)
    give[...] = jnp.where(cfg == 0, high, low).astype(BF16)
    swap = remote(give, got, x_send, x_recv, cfg=1 - cfg)
    swap.start()
    swap.wait_recv()

    a = mine[...].astype(F32)
    b = got[...].astype(F32)
    cond = jnp.where(cfg == 0, a, b)
    uncond = jnp.where(cfg == 0, b, a)
    guided = uncond + GUIDANCE * (cond - uncond)
    live = lax.broadcasted_iota(jnp.int32, (rows, wide), 0) < count
    gl = jnp.where(live, guided, 0.0)
    cl = jnp.where(live, cond, 0.0)
    sums = [jnp.sum(t, axis=0, keepdims=True) for t in (gl, gl * gl, cl, cl * cl)]
    stat[...] = jnp.concatenate(sums + [jnp.zeros((4, wide), F32)], axis=0)
    statbuf[me] = stat[...]

    def st(d):
        return remote(stat, statbuf.at[me], st_send.at[d], st_recv.at[d], seq=lax.rem(me + d, nseq))

    for d in range(1, nseq):
        st(d).start()
    for d in range(1, nseq):
        st(d).wait_recv()
    total = statbuf[0]
    number = cbuf[0][0:1, :]
    for i in range(1, nseq):
        total = total + statbuf[i]
        number = number + cbuf[i][0:1, :]
    number = spread(number, wide)
    g_mean = total[0:1] / number
    g_var = total[1:2] / number - g_mean * g_mean
    c_mean = total[2:3] / number
    c_var = total[3:4] / number - c_mean * c_mean
    factor = RESCALE * jnp.sqrt((c_var + 1.0) / (g_var + 1.0)) + (1.0 - RESCALE)
    vel = g_mean + (guided - g_mean) * factor
    keep = wide - 64
    out_ref[...] = jnp.where(cfg == 0, vel[:, :keep], vel[:, 64:]).astype(BF16)

    def drain(h, _):
        for kind in range(4):
            for s in range(1, last(kind) + 1):
                ring(h, kind, s).wait_send()
            for s in range(0 if kind < 2 else 1, last(kind) + 1):
                d2d(h, kind, s).wait_send()
        for d in range(1, ntp):
            ocopy(h, d).wait_send()
        return 0

    lax.fori_loop(0, heads, drain, 0)
    for d in range(1, nseq):
        cnt(d).wait_send()
        st(d).wait_send()
    for d in range(1, ntp):
        wcopy(d).wait_send()
        wmate(d).wait_send()
    swap.wait_send()


def body(queries, keys, values, text_keys, text_values, prompt_lengths, frame_counts, out_weight):
    rows, width = queries.shape[1:]
    trows = text_keys.shape[1]
    heads = width // HD
    nseq, ntp = lax.axis_size("seq"), lax.axis_size("tp")
    model = out_weight.shape[1]
    cols = model // ntp
    keep = cols // 2
    wide = keep + 64
    cnt_tile = jnp.broadcast_to(frame_counts.astype(F32), (8, HD))
    vm = pl.BlockSpec(memory_space=pltpu.VMEM)
    sm = pl.BlockSpec(memory_space=pltpu.SMEM)
    hbm = pl.BlockSpec(memory_space=pl.ANY)
    dma = pltpu.SemaphoreType.DMA
    return pl.pallas_call(
        functools.partial(kernel, (heads, rows, trows, nseq, ntp, cols)),
        out_shape=jax.ShapeDtypeStruct((rows, keep), BF16),
        in_specs=[sm, sm, vm, vm, vm, vm, vm, vm, hbm],
        out_specs=vm,
        scratch_shapes=[
            pltpu.VMEM((heads, nseq * rows, HD), BF16),
            pltpu.VMEM((heads, nseq * rows, HD), BF16),
            pltpu.VMEM((nseq * rows, HD), BF16),
            pltpu.VMEM((heads, trows, HD), BF16),
            pltpu.VMEM((heads, trows, HD), BF16),
            pltpu.VMEM((trows, HD), BF16),
            pltpu.VMEM((nseq, 8, HD), F32),
            pltpu.VMEM((rows, HD), F32),
            pltpu.VMEM((rows, 2 * HD), F32),
            pltpu.VMEM((heads, ntp, rows, HD), BF16),
            pltpu.VMEM((heads, ntp * HD, cols), BF16),
            pltpu.VMEM((rows, cols), F32),
            pltpu.VMEM((rows, wide), BF16),
            pltpu.VMEM((rows, wide), BF16),
            pltpu.VMEM((rows, wide), BF16),
            pltpu.VMEM((8, wide), F32),
            pltpu.VMEM((nseq, 8, wide), F32),
            dma((heads, 4, 4)), dma((heads, 4, 4)),
            dma((heads, 2, 8)), dma((heads, 2, 8)),
            dma((nseq,)), dma((nseq,)),
            dma((heads, ntp)), dma((heads, ntp)),
            dma((ntp,)), dma((ntp,)), dma((ntp,)), dma((ntp,)), dma,
            dma, dma, dma((nseq,)), dma((nseq,)),
        ],
        compiler_params=pltpu.CompilerParams(
            collective_id=0, has_side_effects=True, vmem_limit_bytes=60 * 1024 * 1024
        ),
    )(
        prompt_lengths, frame_counts, cnt_tile, queries[0], keys[0], values[0],
        text_keys[0], text_values[0], out_weight.reshape(heads, HD, model),
    )


def solution(mesh):
    placed = (
        P("cfg", "seq", "tp"),
        P("cfg", "seq", "tp"),
        P("cfg", "seq", "tp"),
        P("cfg", None, "tp"),
        P("cfg", None, "tp"),
        P("cfg"),
        P("seq"),
        P("tp", None),
    )
    return jax.shard_map(
        body, mesh=mesh, in_specs=placed, out_specs=P("seq", ("tp", "cfg")), check_vma=False
    )
```

time: 328 us -> 174 us (0.53)
  Pallas kernels: 0 us -> 170 us
  waiting for transfers between devices: 131 us -> 0 us
  matrix products: 75.7 us -> 0 us
  local copies, waits for them, and re-layouts: 47.3 us -> 2.46 us
  other arithmetic: 34.9 us -> 0 us
  starting transfers between devices: 22.6 us -> 0 us
  between operations: 15.2 us -> 1.31 us
    pallas_call x0 -> x1, Pallas kernels: none -> 170 us  [body(): pl.pallas_call(functools.partial(kernel, (heads, rows, trows, nseq, ntp,...]
    dot_general x9 -> x0, matrix products: 75.7 us -> none  [the longest x2 34.9 us: attend_block(): jnp.einsum('qhd,khd->hqk', query_heads, key_heads, preferred_element_type...]
    unnamed x4 -> x0, waiting for transfers between devices: 65.5 us -> none
    all_gather x2 -> x0, waiting for transfers between devices: 48.7 us -> none  [the longest x1 48.6 us: body(): key_rows = lax.all_gather(keys[0], 'seq', axis=0, tiled=True)]
    reduce_sum x5 -> x0, other arithmetic: 29 us -> none  [the longest x2 27.8 us: attend_block(): weight_sum = weight_sum * shrink + jnp.sum(weights, axis=2)]
    all_gather x2 -> x0, local copies, waits for them, and re-layouts: 27.5 us -> none  [the longest x1 13.7 us: body(): value_rows = lax.all_gather(values[0], 'seq', axis=0, tiled=True)]
    all_to_all x3 -> x0, starting transfers between devices: 22.6 us -> none  [the longest x2 18.8 us: from_everyone(): lax.all_to_all(jnp.broadcast_to(value[None], (devices, *value.shape)), ax...]
    all_to_all x3 -> x0, waiting for transfers between devices: 17.1 us -> none  [the longest x1 9.53 us: body(): lax.all_to_all(branch, 'cfg', split_axis=2, concat_axis=0, tiled=True)]
  transfers between devices with their start and end apart: 6 -> 0, of which waited for: 5 -> 0; matrix products, arithmetic and copies ran while one was open for 25% -> 0% of each run, Pallas kernels for 0% -> 0%
where the time goes in v1:
time: 174 us; the launch traced here: 173 us
  Pallas kernels  170 us (98%)
  local copies, waits for them, and re-layouts  2.46 us (1%)
    pallas_call x1, Pallas kernels, body(): pl.pallas_call(functools.partial(kernel, (heads, rows, trows, nseq, ntp,...  170 us

profile of v1, /device:TPU:1, one launch (start us, length us, event | category | flops | bytes accessed | tf_op | source)
XLA Modules:
  0.0 173.4 jit_solution(13562305770404779787)
XLA Ops:
  1.3 0.6 broadcast_in_dim.2.cnt_in
  1.9 169.6 %shard_map.82 = bf16[480,320]{1,0:T(8,128)(2,1)} custom-call(s32[1]{0:T(128)S(6)} %copy.10.plen_ref, s32[1]{0:T(128)S(6)} %copy.11.count_ref, f32[8,128]{1,0:T(8,128)} %broadcast_in_dim.2.cnt_in, bf16[480,640]{1,0:T(8,128)(2,1)} %bitcast.10, bf16[480,640]{1,0:T(8,128)(2,1)} %bitcast.11, bf16[480,640]{1,0:T(8,128)(2,1)} %bitcast.12, ...), custom_call_target="tpu_custom_call" | custom-call | tf_op jit(solution)/shard_map/pallas_call | solution.py:345
  171.5 1.9 %copy.9 = bf16[480,320]{0,1:T(8,128)(2,1)} copy(bf16[480,320]{1,0:T(8,128)(2,1)} %shard_map.82) | data formatting | bytes 614400 | tf_op jit(solution)/shard_map/pallas_call | solution.py:345

commit v2 on v1

v2 whole, which is shorter than its diff:
```python
import functools

import jax
import jax.numpy as jnp
from jax import lax
from jax.experimental import pallas as pl
from jax.experimental.pallas import tpu as pltpu
from jax.sharding import PartitionSpec as P

MESH = pl.DeviceIdType.MESH
HD = 128
GUIDANCE = 5.0
RESCALE = 0.7
NEGATIVE = -1e30
LOG2E = 1.4426950408889634
F32 = jnp.float32
BF16 = jnp.bfloat16


def kernel(
    dims,
    plen_ref, count_ref, q_hbm, k_hbm, v_hbm, tk_hbm, tv_hbm, w_hbm,
    out_ref,
    q_ref, k_ref, v_ref, tk_ref, tv_ref, cnt_in,
    kbuf, vbuf, valid, tkbuf, tvbuf, tvalid, cbuf, m_ref, acc, obuf, wbuf,
    oacc, stat, statbuf,
    ring_send, ring_recv, d2d_send, d2d_recv, cnt_send, cnt_recv,
    o_send, o_recv, w_send, w_recv, wd_send, wd_recv, w_loc, in_sem,
    st_send, st_recv,
):
    heads, rows, trows, nseq, ntp, cols = dims
    nz = nseq // 2
    half = rows // 2
    wide = out_ref.shape[1] + 64
    scale = HD ** (-0.5) * LOG2E
    me = lax.axis_index("seq")
    tp = lax.axis_index("tp")
    cfg = lax.axis_index("cfg")
    z = me // 2
    core = lax.rem(me, 2)
    up = lax.rem(z + 1, nz) * 2 + core
    down = lax.rem(z + nz - 1, nz) * 2 + core
    mate = z * 2 + (1 - core)
    nplane = 2 * ntp
    spot = cfg * ntp + tp
    side = 4
    step_a = jnp.where(core == 0, 1, side)
    step_b = jnp.where(core == 0, side, 1)
    pa = lax.rem(spot // step_a, side)
    pb = lax.rem(spot // step_b, side)

    def place(da, db):
        return lax.rem(pa + da + side, side) * step_a + lax.rem(pb + db + side, side) * step_b

    count = count_ref[0]
    plen = plen_ref[0]

    def remote(src, dst, ss, rs, **to):
        return pltpu.make_async_remote_copy(
            src_ref=src, dst_ref=dst, send_sem=ss, recv_sem=rs,
            device_id=to, device_id_type=MESH,
        )

    barrier = pltpu.get_barrier_semaphore()
    for d in range(1, nseq):
        pl.semaphore_signal(barrier, inc=1, device_id={"seq": lax.rem(me + d, nseq)}, device_id_type=MESH)
    for d in range(1, nplane):
        peer = lax.rem(spot + d, nplane)
        pl.semaphore_signal(barrier, inc=1, device_id={"cfg": peer // ntp, "tp": lax.rem(peer, ntp)},
                            device_id_type=MESH)
    loads = [pltpu.make_async_copy(a, b, in_sem.at[i]) for i, (a, b) in enumerate(
        ((k_hbm, k_ref), (v_hbm, v_ref), (tk_hbm, tk_ref), (tv_hbm, tv_ref), (q_hbm, q_ref)))]
    for copy in loads:
        copy.start()
    cnt_in[...] = jnp.broadcast_to(count.astype(F32), cnt_in.shape)
    loads[0].wait()
    loads[1].wait()

    row_id = lax.broadcasted_iota(jnp.int32, (rows, HD), 0)
    trow_id = lax.broadcasted_iota(jnp.int32, (trows, HD), 0)
    scope = jax.named_scope
    for h in range(heads):
        cut = slice(h * HD, (h + 1) * HD)
        kk = k_ref[:, cut].astype(F32)
        vv = v_ref[:, cut].astype(F32)
        kbuf[h, 0:rows, :] = jnp.where(row_id < count, kk, kk[0:1, :]).astype(BF16)
        vbuf[h, 0:rows, :] = jnp.where(row_id < count, vv, 0.0).astype(BF16)

    with scope("entry"):
        pl.semaphore_wait(barrier, nseq - 1 + nplane - 1)

    def slot(kind, s):
        if s == 4:
            return 14
        return 2 + 4 * (s - 1) + (0 if kind < 2 else 2)

    def buf_of(kind):
        return kbuf if kind % 2 == 0 else vbuf

    def at(kind, h, sl):
        return buf_of(kind).at[h, pl.ds(sl * rows, rows), :]

    def last(kind):
        return 4 if kind in (0, 3) else 3

    def ring(h, kind, s):
        src = at(kind, h, 0 if s == 1 else slot(kind, s - 1))
        return remote(src, at(kind, h, slot(kind, s)), ring_send,
                      ring_recv.at[lax.rem(h, 2), kind, s - 1], seq=(up if kind < 2 else down))

    def d2d_index(kind, s):
        if s == 0:
            return 0
        if s == 4:
            return 7
        return s if kind < 2 else 3 + s

    def d2d(h, kind, s):
        sl = 0 if s == 0 else slot(kind, s)
        i = d2d_index(kind, s)
        return remote(at(kind, h, sl), at(kind, h, sl + 1), d2d_send,
                      d2d_recv.at[lax.rem(h, 2), kind % 2, i], seq=mate)

    def launch(h):
        for kind in (0, 2, 1, 3):
            ring(h, kind, 1).start()
        d2d(h, 0, 0).start()
        d2d(h, 1, 0).start()

    def pass_on(h, kind, s):
        if s > last(kind):
            return
        ring(h, kind, s).wait_recv()
        if s < last(kind):
            ring(h, kind, s + 1).start()
        d2d(h, kind, s).start()

    def cnt(d):
        peer = lax.rem(me + d, nseq)
        return remote(cnt_in, cbuf.at[me], cnt_send, cnt_recv, seq=peer)

    def window(owner):
        return pl.ds(pl.multiple_of(owner * cols + cfg * (cols - wide), HD), wide)

    def wcopy(d):
        peer = lax.rem(tp + d, ntp)
        return remote(
            w_hbm.at[:, pl.ds(core * 64, 64), window(peer)],
            wbuf.at[:, pl.ds(tp * HD + core * 64, 64), :],
            w_send, w_recv, tp=peer)

    def wmate(d):
        src = lax.rem(tp + ntp - d, ntp)
        part = wbuf.at[:, pl.ds(src * HD + core * 64, 64), :]
        return remote(part, part, wd_send, wd_recv, seq=mate)

    def bytes_of(ref, sem):
        pltpu.make_async_copy(ref, ref, sem).wait()

    upper, lower = slice(0, half), slice(half, rows)

    def hand(h, da, db, ta, tb, stage, r=None):
        part = obuf.at[h, place(da, db)]
        if r is not None:
            part = obuf.at[h, place(da, db), r, :]
        peer = place(ta, tb)
        remote(part, part, o_send, o_recv.at[h, stage],
               cfg=peer // ntp, tp=lax.rem(peer, ntp)).start()

    def blocks(h, stage, n):
        bytes_of(obuf.at[h, 0:n], o_recv.at[h, stage])

    def relay(h, stage):
        if stage == 0:
            for d in (1, -1):
                hand(h, 0, 0, d, 0, 0)
            for d in (1, -1):
                hand(h, 0, 0, 0, d, 2)
        elif stage == 1:
            blocks(h, 0, 2)
            hand(h, -1, 0, 1, 0, 1, upper)
            hand(h, 1, 0, -1, 0, 1, lower)
            for a in (-1, 1):
                for d in (1, -1):
                    hand(h, a, 0, 0, d, 3)
        elif stage == 2:
            blocks(h, 1, 1)
            for d in (1, -1):
                hand(h, 2, 0, 0, d, 4)
            blocks(h, 2, 2)
            hand(h, 0, -1, 0, 1, 5, upper)
            hand(h, 0, 1, 0, -1, 5, lower)
        elif stage == 3:
            blocks(h, 3, 4)
            for a in (-1, 1):
                hand(h, a, -1, 0, 1, 5, upper)
                hand(h, a, 1, 0, -1, 5, lower)
            blocks(h, 4, 2)
            hand(h, 2, -1, 0, 1, 5, upper)
            hand(h, 2, 1, 0, -1, 5, lower)
        else:
            blocks(h, 5, 4)

    launch(0)
    for d in range(1, nseq):
        cnt(d).start()
    own_w = pltpu.make_async_copy(
        w_hbm.at[:, :, window(tp)],
        wbuf.at[:, pl.ds(tp * HD, HD), :], w_loc)
    own_w.start()
    for d in range(1, ntp):
        wcopy(d).start()

    loads[2].wait()
    loads[3].wait()
    loads[4].wait()
    for h in range(heads):
        cut = slice(h * HD, (h + 1) * HD)
        kk = tk_ref[:, cut].astype(F32)
        vv = tv_ref[:, cut].astype(F32)
        tkbuf[h] = jnp.where(trow_id < plen, kk, kk[0:1, :]).astype(BF16)
        tvbuf[h] = jnp.where(trow_id < plen, vv, 0.0).astype(BF16)
    tvalid[...] = jnp.where(trow_id < plen, 1.0, 0.0).astype(BF16)

    cbuf[me] = jnp.broadcast_to(count.astype(F32), cbuf.shape[1:])
    with scope("first_k"):
        pass_on(0, 0, 1)
        pass_on(0, 2, 1)
    def mark(sl):
        if sl < 2:
            zz, other = z, sl
        elif sl >= 14:
            zz, other = lax.rem(z + 4, nz), sl - 14
        else:
            s, r = 1 + (sl - 2) // 4, (sl - 2) % 4
            zz = lax.rem(z + nz - s, nz) if r < 2 else lax.rem(z + s, nz)
            other = r % 2
        src = zz * 2 + (core if other == 0 else 1 - core)
        c = cbuf[src][0:1, :]
        valid[sl * rows:(sl + 1) * rows, :] = jnp.where(row_id.astype(F32) < c, 1.0, 0.0).astype(BF16)

    def spread(x, n):
        full, rest = divmod(n, HD)
        parts = [x] * full + ([x[:, :rest]] if rest else [])
        return parts[0] if len(parts) == 1 else jnp.concatenate(parts, axis=1)

    def attend(h, part, k, v, ok, first=False):
        r = pl.ds(part * half, half)
        now = lax.rem(h, 2)
        q = q_ref[r, pl.ds(pl.multiple_of(h * HD, HD), HD)]
        s = lax.dot_general(q, k, (((1,), (1,)), ((), ())), preferred_element_type=F32)
        n = s.shape[1]
        mb = jnp.max(s, axis=1, keepdims=True) * scale
        if first:
            m_new = jnp.broadcast_to(mb, (half, HD))
        else:
            m_old = m_ref[now, r, :]
            m_new = jnp.maximum(m_old, mb)
        p = jnp.exp2(s * scale - spread(m_new, n)).astype(BF16)
        pv = lax.dot_general(p, jnp.concatenate([v, ok], axis=1), (((1,), (0,)), ((), ())),
                             preferred_element_type=F32)
        if first:
            acc[now, r, :] = pv
        else:
            shrink = jnp.exp2(m_old - m_new)
            acc[now, r, :] = acc[now, r, :] * jnp.concatenate([shrink, shrink], axis=1) + pv
        m_ref[now, r, :] = m_new

    def attend_slots(h, part, sl, n):
        r = pl.ds(sl * rows, n * rows)
        attend(h, part, kbuf[h, r, :], vbuf[h, r, :], valid[r, :])

    def attend_text(h):
        for part in range(2):
            attend(h, part, tkbuf[h], tvbuf[h], tvalid[...], first=True)

    def project(h):
        for c in range(2):
            lhs = jnp.concatenate([obuf[h, c * ntp + j] for j in range(ntp)], axis=1)
            oacc[c] += jnp.dot(lhs, wbuf[h], preferred_element_type=F32)

    oacc[...] = jnp.zeros_like(oacc)

    attend_text(0)
    with scope("first_v"):
        pass_on(0, 1, 1)
        pass_on(0, 3, 1)
    with scope("counts"):
        bytes_of(cbuf.at[0:nseq - 1], cnt_recv)
    mark(0)
    mark(1)
    d2d(0, 0, 0).wait_recv()
    d2d(0, 1, 0).wait_recv()
    attend_slots(0, 0, 0, 2)

    def head_step(h, _):
        def note(group):
            @pl.when(h == 0)
            def _():
                for sl in range(2 + 4 * group, min(6 + 4 * group, nseq)):
                    mark(sl)

        def k_in(s):
            with scope(f"wk{s}"):
                pass_on(h, 0, s)
                pass_on(h, 2, s)

        def v_in(s):
            with scope(f"wv{s}"):
                pass_on(h, 1, s)
                pass_on(h, 3, s)

        def d_in(s):
            with scope(f"wd{s}"):
                for kind in range(4):
                    if s <= last(kind) and (s < 4 or kind in (0, 3)):
                        d2d(h, kind, s).wait_recv()

        k_in(2)
        attend_slots(h, 1, 0, 2)
        d_in(1)
        note(0)
        attend_slots(h, 0, 2, 4)
        v_in(2)

        @pl.when(h >= 1)
        def _():
            with scope("relay1"):
                relay(h - 1, 1)
        attend_slots(h, 1, 2, 4)

        @pl.when(h == 3)
        def _():
            with scope("ww2"):
                bytes_of(wbuf.at[:, 0:(ntp - 1) * 64, :], wd_recv)
                own_w.wait()

        @pl.when(h >= 3)
        def _():
            with scope("proj"):
                relay(h - 3, 4)
                project(h - 3)
        k_in(3)
        d_in(2)
        note(1)
        attend_slots(h, 0, 6, 4)
        v_in(3)

        @pl.when(h < heads - 1)
        def _():
            launch(h + 1)

        @pl.when(h >= 1)
        def _():
            with scope("relay2"):
                relay(h - 1, 2)
        attend_slots(h, 1, 6, 4)
        d_in(3)
        note(2)
        attend_slots(h, 0, 10, 4)
        k_in(4)
        v_in(4)

        @pl.when(h == 2)
        def _():
            with scope("ww"):
                bytes_of(wbuf.at[:, 0:(ntp - 1) * 64, :], w_recv)
                for d in range(1, ntp):
                    wmate(d).start()

        attend_slots(h, 1, 10, 4)

        @pl.when(h >= 1)
        def _():
            with scope("relay3"):
                relay(h - 1, 3)

        @pl.when(h < heads - 1)
        def _():
            with scope("wk1"):
                pass_on(h + 1, 0, 1)
                pass_on(h + 1, 2, 1)
            attend_text(h + 1)
            d2d(h + 1, 0, 0).wait_recv()
            d2d(h + 1, 1, 0).wait_recv()
            attend_slots(h + 1, 0, 0, 2)
            with scope("wv1"):
                pass_on(h + 1, 1, 1)
                pass_on(h + 1, 3, 1)
        d_in(4)
        note(3)
        now = lax.rem(h, 2)
        for part in range(2):
            attend_slots(h, part, 14, 2)
            r = pl.ds(part * half, half)
            obuf[h, spot, r, :] = (acc[now, r, 0:HD] / acc[now, r, HD:2 * HD]).astype(BF16)
        relay(h, 0)
        return 0

    lax.fori_loop(0, heads, head_step, 0)

    with scope("last1"):
        relay(heads - 1, 1)
    for h in (heads - 3, heads - 2):
        with scope(f"late{h}"):
            relay(h, 4)
        project(h)
    for stage in range(2, 5):
        with scope(f"last{stage}"):
            relay(heads - 1, stage)
    project(heads - 1)

    cond = oacc[0].astype(BF16).astype(F32)
    uncond = oacc[1].astype(BF16).astype(F32)
    guided = uncond + GUIDANCE * (cond - uncond)
    live = lax.broadcasted_iota(jnp.int32, (rows, wide), 0) < count
    gl = jnp.where(live, guided, 0.0)
    cl = jnp.where(live, cond, 0.0)
    sums = [jnp.sum(t, axis=0, keepdims=True) for t in (gl, gl * gl, cl, cl * cl)]
    tiles = wide // HD
    lines = [t[:, i * HD:(i + 1) * HD] for t in sums for i in range(tiles)]
    stat[...] = jnp.concatenate(lines + [jnp.zeros((16 - 4 * tiles, HD), F32)], axis=0)
    statbuf[me] = stat[...]

    def st(d):
        return remote(stat, statbuf.at[me], st_send, st_recv, seq=lax.rem(me + d, nseq))

    for d in range(1, nseq):
        st(d).start()
    with scope("stats"):
        bytes_of(statbuf.at[0:nseq - 1], st_recv)
    total = statbuf[0]
    number = cbuf[0][0:1, :]
    for i in range(1, nseq):
        total = total + statbuf[i]
        number = number + cbuf[i][0:1, :]
    number = spread(number, wide)
    g_sum, g_square, c_sum, c_square = (
        jnp.concatenate([total[j * tiles + i:j * tiles + i + 1] for i in range(tiles)], axis=1)
        for j in range(4))
    g_mean = g_sum / number
    g_var = g_square / number - g_mean * g_mean
    c_mean = c_sum / number
    c_var = c_square / number - c_mean * c_mean
    factor = RESCALE * jnp.sqrt((c_var + 1.0) / (g_var + 1.0)) + (1.0 - RESCALE)
    vel = g_mean + (guided - g_mean) * factor
    keep = wide - 64
    out_ref[...] = jnp.where(cfg == 0, vel[:, :keep], vel[:, 64:]).astype(BF16)

    with scope("drain"):
        bytes_of(kbuf.at[:, 0:14 * rows, :], ring_send)
        bytes_of(kbuf, d2d_send)
        bytes_of(obuf.at[:, 0:nplane - 1], o_send)
        bytes_of(cbuf.at[0:nseq - 1], cnt_send)
        bytes_of(statbuf.at[0:nseq - 1], st_send)
        bytes_of(wbuf.at[:, 0:(ntp - 1) * 64, :], w_send)
        bytes_of(wbuf.at[:, 0:(ntp - 1) * 64, :], wd_send)


def body(queries, keys, values, text_keys, text_values, prompt_lengths, frame_counts, out_weight):
    rows, width = queries.shape[1:]
    trows = text_keys.shape[1]
    heads = width // HD
    nseq, ntp = lax.axis_size("seq"), lax.axis_size("tp")
    model = out_weight.shape[1]
    cols = model // ntp
    keep = cols // 2
    wide = keep + 64
    vm = pl.BlockSpec(memory_space=pltpu.VMEM)
    sm = pl.BlockSpec(memory_space=pltpu.SMEM)
    hbm = pl.BlockSpec(memory_space=pl.ANY)
    dma = pltpu.SemaphoreType.DMA
    return pl.pallas_call(
        functools.partial(kernel, (heads, rows, trows, nseq, ntp, cols)),
        out_shape=jax.ShapeDtypeStruct((rows, keep), BF16),
        in_specs=[sm, sm, hbm, hbm, hbm, hbm, hbm, hbm],
        out_specs=vm,
        scratch_shapes=[
            pltpu.VMEM((rows, width), BF16),
            pltpu.VMEM((rows, width), BF16),
            pltpu.VMEM((rows, width), BF16),
            pltpu.VMEM((trows, width), BF16),
            pltpu.VMEM((trows, width), BF16),
            pltpu.VMEM((8, HD), F32),
            pltpu.VMEM((heads, nseq * rows, HD), BF16),
            pltpu.VMEM((heads, nseq * rows, HD), BF16),
            pltpu.VMEM((nseq * rows, HD), BF16),
            pltpu.VMEM((heads, trows, HD), BF16),
            pltpu.VMEM((heads, trows, HD), BF16),
            pltpu.VMEM((trows, HD), BF16),
            pltpu.VMEM((nseq, 8, HD), F32),
            pltpu.VMEM((2, rows, HD), F32),
            pltpu.VMEM((2, rows, 2 * HD), F32),
            pltpu.VMEM((heads, 2 * ntp, rows, HD), BF16),
            pltpu.VMEM((heads, ntp * HD, wide), BF16),
            pltpu.VMEM((2, rows, wide), F32),
            pltpu.VMEM((16, HD), F32),
            pltpu.VMEM((nseq, 16, HD), F32),
            dma, dma((2, 4, 4)), dma, dma((2, 2, 8)), dma, dma,
            dma, dma((heads, 6)), dma, dma, dma, dma, dma, dma((5,)),
            dma, dma,
        ],
        compiler_params=pltpu.CompilerParams(
            collective_id=0, has_side_effects=True, vmem_limit_bytes=60 * 1024 * 1024
        ),
    )(
        prompt_lengths, frame_counts, queries[0], keys[0], values[0],
        text_keys[0], text_values[0], out_weight.reshape(heads, HD, model),
    )


def solution(mesh):
    placed = (
        P("cfg", "seq", "tp"),
        P("cfg", "seq", "tp"),
        P("cfg", "seq", "tp"),
        P("cfg", None, "tp"),
        P("cfg", None, "tp"),
        P("cfg"),
        P("seq"),
        P("tp", None),
    )
    return jax.shard_map(
        body, mesh=mesh, in_specs=placed, out_specs=P("seq", ("tp", "cfg")), check_vma=False
    )
```

time: 174 us -> 147 us (0.84)
  Pallas kernels: 170 us -> 144 us
    pallas_call x1, Pallas kernels: 170 us -> 144 us  [body(): pl.pallas_call(functools.partial(kernel, (heads, rows, trows, nseq, ntp,...]
where the time goes in v2:
time: 147 us
  Pallas kernels  144 us (98%)
  local copies, waits for them, and re-layouts  1.87 us (1%)
    pallas_call x1, Pallas kernels, body(): pl.pallas_call(functools.partial(kernel, (heads, rows, trows, nseq, ntp,...  144 us

profile of v2, /device:TPU:1, one launch (start us, length us, event | category | flops | bytes accessed | tf_op | source)
XLA Modules:
  0.0 147.1 jit_solution(54323973279650084)
XLA Ops:
  1.3 143.9 %shard_map.82 = bf16[480,320]{1,0:T(8,128)(2,1)} custom-call(s32[1]{0:T(128)S(6)} %copy.10.plen_ref, s32[1]{0:T(128)S(6)} %copy.11.count_ref, bf16[480,640]{1,0:T(8,128)(2,1)} %bitcast.9, bf16[480,640]{1,0:T(8,128)(2,1)} %bitcast.10, bf16[480,640]{1,0:T(8,128)(2,1)} %bitcast.11, bf16[512,640]{1,0:T(8,128)(2,1)} %bitcast.7, bf16[512,640]{1,0:T(8,128)(2,1)} %bitcast.8, ...), custom_call_target="tpu_custom_call" | custom-call | tf_op jit(solution)/shard_map/pallas_call | solution.py:473
  145.2 1.9 %copy.9 = bf16[480,320]{0,1:T(8,128)(2,1)} copy(bf16[480,320]{1,0:T(8,128)(2,1)} %shard_map.82) | data formatting | bytes 614400 | tf_op jit(solution)/shard_map/pallas_call | solution.py:473

commit v3 on v2

--- a/solution.py
+++ b/solution.py
@@ -121,8 +121,11 @@
         return remote(at(kind, h, sl), at(kind, h, sl + 1), d2d_send,
                       d2d_recv.at[lax.rem(h, 2), kind % 2, i], seq=mate)
 
-    def launch(h):
-        for kind in (0, 2, 1, 3):
+    def launch(h, ahead):
+        if ahead:
+            ring(h, 2, 1).start()
+            return
+        for kind in (0, 1, 3):
             ring(h, kind, 1).start()
         d2d(h, 0, 0).start()
         d2d(h, 1, 0).start()
@@ -137,7 +140,7 @@
 
     def cnt(d):
         peer = lax.rem(me + d, nseq)
-        return remote(cnt_in, cbuf.at[me], cnt_send, cnt_recv, seq=peer)
+        return remote(cnt_in.at[0:1, :], cbuf.at[me, 0:1, :], cnt_send, cnt_recv, seq=peer)
 
     def window(owner):
         return pl.ds(pl.multiple_of(owner * cols + cfg * (cols - wide), HD), wide)
@@ -183,13 +186,13 @@
             for a in (-1, 1):
                 for d in (1, -1):
                     hand(h, a, 0, 0, d, 3)
+            blocks(h, 2, 2)
+            hand(h, 0, -1, 0, 1, 5, upper)
+            hand(h, 0, 1, 0, -1, 5, lower)
         elif stage == 2:
             blocks(h, 1, 1)
             for d in (1, -1):
                 hand(h, 2, 0, 0, d, 4)
-            blocks(h, 2, 2)
-            hand(h, 0, -1, 0, 1, 5, upper)
-            hand(h, 0, 1, 0, -1, 5, lower)
         elif stage == 3:
             blocks(h, 3, 4)
             for a in (-1, 1):
@@ -201,9 +204,10 @@
         else:
             blocks(h, 5, 4)
 
-    launch(0)
     for d in range(1, nseq):
         cnt(d).start()
+    launch(0, True)
+    launch(0, False)
     own_w = pltpu.make_async_copy(
         w_hbm.at[:, :, window(tp)],
         wbuf.at[:, pl.ds(tp * HD, HD), :], w_loc)
@@ -286,7 +290,7 @@
         pass_on(0, 1, 1)
         pass_on(0, 3, 1)
     with scope("counts"):
-        bytes_of(cbuf.at[0:nseq - 1], cnt_recv)
+        bytes_of(cbuf.at[0:nseq - 1, 0:1, :], cnt_recv)
     mark(0)
     mark(1)
     d2d(0, 0, 0).wait_recv()
@@ -303,7 +307,8 @@
         def k_in(s):
             with scope(f"wk{s}"):
                 pass_on(h, 0, s)
-                pass_on(h, 2, s)
+                if s < 4:
+                    pass_on(h, 2, s)
 
         def v_in(s):
             with scope(f"wv{s}"):
@@ -329,18 +334,22 @@
                 relay(h - 1, 1)
         attend_slots(h, 1, 2, 4)
 
-        @pl.when(h == 3)
+        @pl.when(h == 2)
         def _():
             with scope("ww2"):
                 bytes_of(wbuf.at[:, 0:(ntp - 1) * 64, :], wd_recv)
                 own_w.wait()
 
-        @pl.when(h >= 3)
+        @pl.when(h >= 2)
         def _():
             with scope("proj"):
-                relay(h - 3, 4)
-                project(h - 3)
+                relay(h - 2, 4)
+                project(h - 2)
         k_in(3)
+
+        @pl.when(h < heads - 1)
+        def _():
+            launch(h + 1, True)
         d_in(2)
         note(1)
         attend_slots(h, 0, 6, 4)
@@ -348,7 +357,7 @@
 
         @pl.when(h < heads - 1)
         def _():
-            launch(h + 1)
+            launch(h + 1, False)
 
         @pl.when(h >= 1)
         def _():
@@ -359,9 +368,18 @@
         note(2)
         attend_slots(h, 0, 10, 4)
         k_in(4)
-        v_in(4)
-
-        @pl.when(h == 2)
+
+        @pl.when(h < heads - 1)
+        def _():
+            with scope("wk1d"):
+                pass_on(h + 1, 2, 1)
+
+        @pl.when(h == heads - 1)
+        def _():
+            with scope("wv4"):
+                pass_on(h, 3, 4)
+
+        @pl.when(h == 1)
         def _():
             with scope("ww"):
                 bytes_of(wbuf.at[:, 0:(ntp - 1) * 64, :], w_recv)
@@ -379,7 +397,7 @@
         def _():
             with scope("wk1"):
                 pass_on(h + 1, 0, 1)
-                pass_on(h + 1, 2, 1)
+                pass_on(h, 3, 4)
             attend_text(h + 1)
             d2d(h + 1, 0, 0).wait_recv()
             d2d(h + 1, 1, 0).wait_recv()
@@ -401,10 +419,9 @@
 
     with scope("last1"):
         relay(heads - 1, 1)
-    for h in (heads - 3, heads - 2):
-        with scope(f"late{h}"):
-            relay(h, 4)
-        project(h)
+    with scope("late"):
+        relay(heads - 2, 4)
+    project(heads - 2)
     for stage in range(2, 5):
         with scope(f"last{stage}"):
             relay(heads - 1, stage)
@@ -451,7 +468,7 @@
         bytes_of(kbuf.at[:, 0:14 * rows, :], ring_send)
         bytes_of(kbuf, d2d_send)
         bytes_of(obuf.at[:, 0:nplane - 1], o_send)
-        bytes_of(cbuf.at[0:nseq - 1], cnt_send)
+        bytes_of(cbuf.at[0:nseq - 1, 0:1, :], cnt_send)
         bytes_of(statbuf.at[0:nseq - 1], st_send)
         bytes_of(wbuf.at[:, 0:(ntp - 1) * 64, :], w_send)
         bytes_of(wbuf.at[:, 0:(ntp - 1) * 64, :], wd_send)

time: 147 us -> 141 us (0.959)
  Pallas kernels: 144 us -> 138 us
    pallas_call x1, Pallas kernels: 144 us -> 138 us  [body(): pl.pallas_call(functools.partial(kernel, (heads, rows, trows, nseq, ntp,...]
where the time goes in v3:
time: 141 us
  Pallas kernels  138 us (98%)
  local copies, waits for them, and re-layouts  1.87 us (1%)
    pallas_call x1, Pallas kernels, body(): pl.pallas_call(functools.partial(kernel, (heads, rows, trows, nseq, ntp,...  138 us

profile of v3, /device:TPU:1, one launch (start us, length us, event | category | flops | bytes accessed | tf_op | source)
XLA Modules:
  0.0 141.2 jit_solution(7697024628504477454)
XLA Ops:
  1.3 138.0 %shard_map.82 = bf16[480,320]{1,0:T(8,128)(2,1)} custom-call(s32[1]{0:T(128)S(6)} %copy.10.plen_ref, s32[1]{0:T(128)S(6)} %copy.11.count_ref, bf16[480,640]{1,0:T(8,128)(2,1)} %bitcast.9, bf16[480,640]{1,0:T(8,128)(2,1)} %bitcast.10, bf16[480,640]{1,0:T(8,128)(2,1)} %bitcast.11, bf16[512,640]{1,0:T(8,128)(2,1)} %bitcast.7, bf16[512,640]{1,0:T(8,128)(2,1)} %bitcast.8, ...), custom_call_target="tpu_custom_call" | custom-call | tf_op jit(solution)/shard_map/pallas_call | solution.py:490
  139.3 1.9 %copy.9 = bf16[480,320]{0,1:T(8,128)(2,1)} copy(bf16[480,320]{1,0:T(8,128)(2,1)} %shard_map.82) | data formatting | bytes 614400 | tf_op jit(solution)/shard_map/pallas_call | solution.py:490

commit v4 on v2

v4 whole, which is shorter than its diff:
```python
import functools

import jax
import jax.numpy as jnp
from jax import lax
from jax.experimental import pallas as pl
from jax.experimental.pallas import tpu as pltpu
from jax.sharding import PartitionSpec as P

MESH = pl.DeviceIdType.MESH
HD = 128
GUIDANCE = 5.0
RESCALE = 0.7
NEGATIVE = -1e30
LOG2E = 1.4426950408889634
F32 = jnp.float32
BF16 = jnp.bfloat16


def kernel(
    dims,
    plen_ref, count_ref, q_hbm, k_hbm, v_hbm, tk_hbm, tv_hbm, w_hbm,
    out_ref,
    k_ref, v_ref, tk_ref, tv_ref, cnt_in, qout, kvout, qhome, qring,
    kvh, kvr, valid_h, valid_r, tkv, tvalid, cbuf, m_ref, acc, oback, obuf, wbuf,
    oacc, stat, statbuf,
    q_send, q_recv, kv_send, kv_recv, kb_recv, kd_send, kd_recv, kbd_recv,
    ring_send, ring_recv, d2d_send, d2d_recv, cnt_send, cnt_recv, back_send, back_recv,
    o_send, o_recv, w_send, w_recv, wd_send, wd_recv, w_loc, in_sem,
    st_send, st_recv,
):
    heads, rows, trows, nseq, ntp, cols = dims
    nz = nseq // 2
    units = 4
    half = rows // 2
    wide = out_ref.shape[1] + 64
    scale = HD ** (-0.5) * LOG2E
    me = lax.axis_index("seq")
    tp = lax.axis_index("tp")
    cfg = lax.axis_index("cfg")
    z = me // 2
    core = lax.rem(me, 2)
    odd = lax.rem(z, 2)
    up = lax.rem(z + 1, nz) * 2 + core
    down = lax.rem(z + nz - 1, nz) * 2 + core
    mate = z * 2 + (1 - core)
    buddy = (z + 1 - 2 * odd) * 2 + core
    nplane = 2 * ntp
    spot = cfg * ntp + tp
    side = 4
    step_a = jnp.where(core == 0, 1, side)
    step_b = jnp.where(core == 0, side, 1)
    pa = lax.rem(spot // step_a, side)
    pb = lax.rem(spot // step_b, side)

    def place(da, db):
        return lax.rem(pa + da + side, side) * step_a + lax.rem(pb + db + side, side) * step_b

    def target(u):
        flip = lax.rem(odd + u, 2)
        return lax.rem(z + nz + u * (1 - 2 * flip), nz)

    def owner(u):
        return lax.rem(z + nz + u * (2 * odd - 1), nz)

    def other_owner(u):
        return lax.rem(z + nz - (1 + u) * (2 * odd - 1), nz)

    def head_of(u):
        return target(u) // 2 if u else z // 2

    def lanes(h):
        return pl.ds(pl.multiple_of(h * HD, HD), HD)

    count = count_ref[0]
    plen = plen_ref[0]
    scope = jax.named_scope

    def remote(src, dst, ss, rs, **to):
        return pltpu.make_async_remote_copy(
            src_ref=src, dst_ref=dst, send_sem=ss, recv_sem=rs,
            device_id=to, device_id_type=MESH,
        )

    def bytes_of(ref, sem):
        pltpu.make_async_copy(ref, ref, sem).wait()

    barrier = pltpu.get_barrier_semaphore()
    for d in range(1, nseq):
        pl.semaphore_signal(barrier, inc=1, device_id={"seq": lax.rem(me + d, nseq)}, device_id_type=MESH)
    for d in range(1, nplane):
        peer = lax.rem(spot + d, nplane)
        pl.semaphore_signal(barrier, inc=1, device_id={"cfg": peer // ntp, "tp": lax.rem(peer, ntp)},
                            device_id_type=MESH)
    pairs = [(k_hbm, k_ref), (v_hbm, v_ref), (tk_hbm, tk_ref), (tv_hbm, tv_ref),
             (q_hbm.at[:, lanes(head_of(0))], qhome.at[0]),
             (q_hbm.at[:, lanes(heads - 1)], qring)]
    pairs += [(q_hbm.at[:, lanes(head_of(u))], qout.at[u - 1]) for u in range(1, units)]
    loads = [pltpu.make_async_copy(a, b, in_sem.at[i]) for i, (a, b) in enumerate(pairs)]
    for copy in loads:
        copy.start()
    cnt_in[...] = jnp.broadcast_to(count.astype(F32), cnt_in.shape)
    loads[0].wait()
    loads[1].wait()

    row_id = lax.broadcasted_iota(jnp.int32, (rows, HD), 0)
    trow_id = lax.broadcasted_iota(jnp.int32, (trows, HD), 0)
    for u in range(units + 1):
        cut = lanes(head_of(u) if u < units else heads - 1)
        kk = k_ref[:, cut].astype(F32)
        vv = v_ref[:, cut].astype(F32)
        kk = jnp.where(row_id < count, kk, kk[0:1, :]).astype(BF16)
        vv = jnp.where(row_id < count, vv, 0.0).astype(BF16)
        if u == 0:
            kvh[0, 0:rows, :] = kk
            kvh[1, 0:rows, :] = vv
        elif u < units:
            kvout[u - 1, 0] = kk
            kvout[u - 1, 1] = vv
        else:
            kvr[0, 0:rows, :] = kk
            kvr[1, 0:rows, :] = vv
    for copy in loads[4:]:
        copy.wait()

    with scope("entry"):
        pl.semaphore_wait(barrier, nseq - 1 + nplane - 1)

    def hslot(i):
        return kvh.at[:, pl.ds(i * rows, rows), :]

    def q_out(u):
        return remote(qout.at[u - 1], qhome.at[u], q_send, q_recv.at[u - 1], seq=target(u) * 2 + core)

    def kv_out(u):
        return remote(kvout.at[u - 1], hslot(4 * u), kv_send, kv_recv.at[u - 1], seq=target(u) * 2 + core)

    def kv_buddy(u):
        return remote(hslot(4 * u), hslot(4 * u + 2), kv_send, kb_recv.at[u], seq=buddy)

    def kv_mate(u):
        return remote(hslot(4 * u), hslot(4 * u + 1), kd_send, kd_recv.at[u], seq=mate)

    def kv_buddy_mate(u):
        return remote(hslot(4 * u + 2), hslot(4 * u + 3), kd_send, kbd_recv.at[u], seq=mate)

    def o_back(u):
        return remote(oback.at[u - 1], obuf.at[u, spot], back_send, back_recv.at[u - 1], seq=owner(u) * 2 + core)

    def slot(kind, s):
        if s == 4:
            return 14
        return 2 + 4 * (s - 1) + (0 if kind < 2 else 2)

    def at(kind, sl):
        return kvr.at[kind % 2, pl.ds(sl * rows, rows), :]

    def last(kind):
        return 4 if kind in (0, 3) else 3

    def ring(kind, s):
        src = at(kind, 0 if s == 1 else slot(kind, s - 1))
        return remote(src, at(kind, slot(kind, s)), ring_send,
                      ring_recv.at[kind, s - 1], seq=(up if kind < 2 else down))

    def d2d(kind, s):
        sl = 0 if s == 0 else slot(kind, s)
        i = {0: 0, 4: 7}.get(s, s if kind < 2 else 3 + s)
        return remote(at(kind, sl), at(kind, sl + 1), d2d_send,
                      d2d_recv.at[kind % 2, i], seq=mate)

    def pass_on(kind, s):
        if s > last(kind):
            return
        ring(kind, s).wait_recv()
        if s < last(kind):
            ring(kind, s + 1).start()
        d2d(kind, s).start()

    def d_in(s):
        for kind in range(4):
            if s <= last(kind) and (s < 4 or kind in (0, 3)):
                d2d(kind, s).wait_recv()

    def cnt(d):
        peer = lax.rem(me + d, nseq)
        return remote(cnt_in.at[0:1, :], cbuf.at[me, 0:1, :], cnt_send, cnt_recv, seq=peer)

    def window(who):
        return pl.ds(pl.multiple_of(who * cols + cfg * (cols - wide), HD), wide)

    def wcopy(d):
        peer = lax.rem(tp + d, ntp)
        return remote(
            w_hbm.at[:, pl.ds(core * 64, 64), window(peer)],
            wbuf.at[:, pl.ds(tp * HD + core * 64, 64), :],
            w_send, w_recv, tp=peer)

    def wmate(d):
        src = lax.rem(tp + ntp - d, ntp)
        part = wbuf.at[:, pl.ds(src * HD + core * 64, 64), :]
        return remote(part, part, wd_send, wd_recv, seq=mate)

    upper, lower = slice(0, half), slice(half, rows)

    def hand(u, da, db, ta, tb, stage, r=None):
        part = obuf.at[u, place(da, db)]
        if r is not None:
            part = obuf.at[u, place(da, db), r, :]
        peer = place(ta, tb)
        remote(part, part, o_send, o_recv.at[u, stage],
               cfg=peer // ntp, tp=lax.rem(peer, ntp)).start()

    def blocks(u, stage, n):
        bytes_of(obuf.at[u, 0:n], o_recv.at[u, stage])

    def relay(u, stage):
        with scope(f"R{u}{stage}"):
            relay_step(u, stage)

    def relay_step(u, stage):
        if stage == 0:
            if 0 < u < units:
                o_back(u).wait_recv()
            for d in (1, -1):
                hand(u, 0, 0, d, 0, 0)
            for d in (1, -1):
                hand(u, 0, 0, 0, d, 2)
        elif stage == 1:
            blocks(u, 0, 2)
            hand(u, -1, 0, 1, 0, 1, upper)
            hand(u, 1, 0, -1, 0, 1, lower)
            for a in (-1, 1):
                for d in (1, -1):
                    hand(u, a, 0, 0, d, 3)
            blocks(u, 2, 2)
            hand(u, 0, -1, 0, 1, 5, upper)
            hand(u, 0, 1, 0, -1, 5, lower)
        elif stage == 2:
            blocks(u, 1, 1)
            for d in (1, -1):
                hand(u, 2, 0, 0, d, 4)
        elif stage == 3:
            blocks(u, 3, 4)
            for a in (-1, 1):
                hand(u, a, -1, 0, 1, 5, upper)
                hand(u, a, 1, 0, -1, 5, lower)
            blocks(u, 4, 2)
            hand(u, 2, -1, 0, 1, 5, upper)
            hand(u, 2, 1, 0, -1, 5, lower)
        else:
            blocks(u, 5, 4)

    for d in range(1, nseq):
        cnt(d).start()
    kv_buddy(0).start()
    q_out(1).start()
    kv_out(1).start()
    kv_mate(0).start()
    kv_out(2).start()
    kv_out(3).start()
    own_w = pltpu.make_async_copy(
        w_hbm.at[:, :, window(tp)],
        wbuf.at[:, pl.ds(tp * HD, HD), :], w_loc)

    loads[2].wait()
    loads[3].wait()
    for i in range(2):
        cut = lanes(head_of(0) if i == 0 else heads - 1)
        kk = tk_ref[:, cut].astype(F32)
        vv = tv_ref[:, cut].astype(F32)
        tkv[i, 0] = jnp.where(trow_id < plen, kk, kk[0:1, :]).astype(BF16)
        tkv[i, 1] = jnp.where(trow_id < plen, vv, 0.0).astype(BF16)
    tvalid[...] = jnp.where(trow_id < plen, 1.0, 0.0).astype(BF16)
    cbuf[me] = jnp.broadcast_to(count.astype(F32), cbuf.shape[1:])

    def mark(buf, sl, src):
        c = cbuf[src][0:1, :]
        buf[sl * rows:(sl + 1) * rows, :] = jnp.where(row_id.astype(F32) < c, 1.0, 0.0).astype(BF16)

    def mark_home(u):
        for i, zz in enumerate((owner(u), owner(u), other_owner(u), other_owner(u))):
            mark(valid_h, 4 * u + i, zz * 2 + (core if i % 2 == 0 else 1 - core))

    def mark_ring(sl):
        if sl < 2:
            zz, other = z, sl
        elif sl >= 14:
            zz, other = lax.rem(z + 4, nz), sl - 14
        else:
            s, r = 1 + (sl - 2) // 4, (sl - 2) % 4
            zz = lax.rem(z + nz - s, nz) if r < 2 else lax.rem(z + s, nz)
            other = r % 2
        mark(valid_r, sl, zz * 2 + (core if other == 0 else 1 - core))

    def spread(x, n):
        full, rest = divmod(n, HD)
        parts = [x] * full + ([x[:, :rest]] if rest else [])
        return parts[0] if len(parts) == 1 else jnp.concatenate(parts, axis=1)

    def attend(u, tiles, first=False):
        q = qring[...] if isinstance(u, int) and u == units else qhome[u]
        held = None
        for tile in [*tiles, None]:
            fresh = None
            if tile is not None:
                k, v, ok = tile
                fresh = (v, ok, lax.dot_general(q, k, (((1,), (1,)), ((), ())), preferred_element_type=F32))
            if held is not None:
                v, ok, s = held
                n = s.shape[1]
                mb = jnp.max(s, axis=1, keepdims=True) * scale
                if first:
                    m_new = jnp.broadcast_to(mb, (rows, HD))
                else:
                    m_old = m_ref[u]
                    m_new = jnp.maximum(m_old, mb)
                p = jnp.exp2(s * scale - spread(m_new, n)).astype(BF16)
                pv = lax.dot_general(p, jnp.concatenate([v, ok], axis=1), (((1,), (0,)), ((), ())),
                                     preferred_element_type=F32)
                if first:
                    acc[u] = pv
                else:
                    shrink = jnp.exp2(m_old - m_new)
                    acc[u] = acc[u] * jnp.concatenate([shrink, shrink], axis=1) + pv
                m_ref[u] = m_new
            held = fresh

    def text(u):
        i = 1 if isinstance(u, int) and u == units else 0
        attend(u, [(tkv[i, 0], tkv[i, 1], tvalid[...])], first=True)

    def cuts(kv, ok, start, n):
        done, out = 0, []
        while done < n * rows:
            size = min(1024 if n > 2 else 512, n * rows - done)
            r = pl.ds(pl.multiple_of(start * rows + done, 32), size)
            out.append((kv[0, r, :], kv[1, r, :], ok[r, :]))
            done += size
        return out

    def group(u, g):
        attend(u, cuts(kvh, valid_h, 4 * g, 4))

    def stretch(sl, n):
        attend(units, cuts(kvr, valid_r, sl, n))

    def finish(u, put):
        for part in range(2):
            r = pl.ds(part * half, half)
            put(r, (acc[u, r, 0:HD] / acc[u, r, HD:2 * HD]).astype(BF16))

    def to_obuf(u):
        def put(r, x):
            obuf[u, spot, r, :] = x
        finish(u, put)

    def to_owner(u):
        def put(r, x):
            oback[u - 1, r, :] = x
        finish(u, put)
        o_back(u).start()

    def project(u):
        h = head_of(u) if u < units else heads - 1
        with scope(f"proj{u}"):
            for c in range(2):
                lhs = jnp.concatenate([obuf[u, c * ntp + j] for j in range(ntp)], axis=1)
                oacc[c] += jnp.dot(lhs, wbuf[h], preferred_element_type=F32)

    def arrive(u):
        with scope(f"kv{u}"):
            kv_out(u).wait_recv()
            kv_buddy(u).start()
            kv_mate(u).start()

    def arrive_buddy(u):
        with scope(f"kb{u}"):
            kv_buddy(u).wait_recv()
            kv_buddy_mate(u).start()

    def ready(u):
        with scope(f"kd{u}"):
            kv_mate(u).wait_recv()
            kv_buddy_mate(u).wait_recv()

    oacc[...] = jnp.zeros_like(oacc)
    text(0)
    with scope("counts"):
        bytes_of(cbuf.at[0:nseq - 1, 0:1, :], cnt_recv)
    mark_home(0)
    arrive_buddy(0)

    def hop(s, which):
        with scope(f"{'kv'[which]}r{s}"):
            pass_on(which, s)
            pass_on(2 + which, s)

    def wait_q(u):
        with scope(f"q{u}"):
            q_out(u).wait_recv()

    def weights_out():
        own_w.start()
        for d in range(1, ntp):
            wcopy(d).start()

    def weights_in():
        with scope("ww"):
            bytes_of(wbuf.at[:, 0:(ntp - 1) * 64, :], w_recv)
            for d in range(1, ntp):
                wmate(d).start()

    def launch():
        ring(0, 1).start()
        ring(2, 1).start()
        ring(1, 1).start()
        ring(3, 1).start()
        d2d(0, 0).start()
        d2d(1, 0).start()

    def x4():
        with scope("x4"):
            pass_on(0, 4)
            pass_on(3, 4)

    order = [(0, 0), (1, 0), (0, 1), (1, 1), (0, 2), (1, 2), (0, 3), (1, 3),
             (2, 0), (2, 1), (2, 2), (2, 3), (3, 0), (3, 1), (3, 2), (3, 3)]
    ahead = {
        0: [lambda: arrive(1), lambda: ready(0)],
        1: [weights_out, lambda: wait_q(1), lambda: mark_home(1)],
        2: [lambda: arrive(2), lambda: arrive_buddy(1), lambda: arrive(3), lambda: ready(1)],
        3: [lambda: mark_home(2)],
        4: [lambda: arrive_buddy(2), q_out(2).start, lambda: ready(2)],
        5: [lambda: mark_home(3)],
        6: [lambda: arrive_buddy(3), q_out(3).start, lambda: ready(3)],
        7: [lambda: to_obuf(0), lambda: relay(0, 0)],
        8: [lambda: to_owner(1), launch, lambda: wait_q(2)],
        9: [lambda: relay(0, 1)],
        10: [lambda: relay(1, 0), weights_in],
        11: [lambda: relay(0, 2), lambda: hop(1, 0)],
        12: [lambda: to_owner(2), lambda: wait_q(3)],
        13: [lambda: relay(0, 3), lambda: hop(1, 1)],
        14: [lambda: relay(1, 1)],
        15: [lambda: hop(2, 0)],
    }

    def work(k, _):
        for j, steps in ahead.items():
            @pl.when(k == j)
            def _(steps=steps):
                for step in steps:
                    step()
        u, g = jnp.int32(0), jnp.int32(0)
        for j, (a, b) in enumerate(order):
            u = jnp.where(k == j, a, u)
            g = jnp.where(k == j, b, g)

        @pl.when((g == 0) & (k > 0))
        def _():
            text(u)
        group(u, g)
        return 0

    lax.fori_loop(0, len(order), work, 0)
    to_owner(3)
    relay(2, 0)
    relay(1, 2)
    hop(2, 1)
    text(units)
    hop(3, 0)
    d2d(0, 0).wait_recv()
    d2d(1, 0).wait_recv()
    for sl in range(2):
        mark_ring(sl)
    stretch(0, 2)
    relay(1, 3)
    relay(2, 1)
    hop(3, 1)

    def far(s, _):
        @pl.when(s == 0)
        def _():
            d_in(1)
            for sl in range(2, 6):
                mark_ring(sl)

        @pl.when(s == 1)
        def _():
            relay(3, 0)
            d_in(2)
            for sl in range(6, 10):
                mark_ring(sl)

        @pl.when(s == 2)
        def _():
            x4()
            relay(2, 2)
            d_in(3)
            for sl in range(10, 16):
                mark_ring(sl)
        stretch(2 + 4 * s, 4)
        return 0

    lax.fori_loop(0, 3, far, 0)
    with scope("ww2"):
        bytes_of(wbuf.at[:, 0:(ntp - 1) * 64, :], wd_recv)
        own_w.wait()
    d_in(4)
    stretch(14, 2)
    to_obuf(units)
    relay(units, 0)
    relay(0, 4)
    project(0)
    relay(3, 1)
    relay(2, 3)
    relay(1, 4)
    project(1)
    relay(3, 2)
    relay(units, 1)
    relay(3, 3)
    relay(2, 4)
    project(2)
    relay(units, 2)
    relay(units, 3)
    relay(3, 4)
    project(3)
    relay(units, 4)
    project(units)

    cond = oacc[0].astype(BF16).astype(F32)
    uncond = oacc[1].astype(BF16).astype(F32)
    guided = uncond + GUIDANCE * (cond - uncond)
    live = lax.broadcasted_iota(jnp.int32, (rows, wide), 0) < count
    gl = jnp.where(live, guided, 0.0)
    cl = jnp.where(live, cond, 0.0)
    sums = [jnp.sum(t, axis=0, keepdims=True) for t in (gl, gl * gl, cl, cl * cl)]
    tiles = wide // HD
    lines = [t[:, i * HD:(i + 1) * HD] for t in sums for i in range(tiles)]
    stat[...] = jnp.concatenate(lines + [jnp.zeros((16 - 4 * tiles, HD), F32)], axis=0)
    statbuf[me] = stat[...]

    def st(d):
        return remote(stat, statbuf.at[me], st_send, st_recv, seq=lax.rem(me + d, nseq))

    for d in range(1, nseq):
        st(d).start()
    with scope("stats"):
        bytes_of(statbuf.at[0:nseq - 1], st_recv)
    total = statbuf[0]
    number = cbuf[0][0:1, :]
    for i in range(1, nseq):
        total = total + statbuf[i]
        number = number + cbuf[i][0:1, :]
    number = spread(number, wide)
    g_sum, g_square, c_sum, c_square = (
        jnp.concatenate([total[j * tiles + i:j * tiles + i + 1] for i in range(tiles)], axis=1)
        for j in range(4))
    g_mean = g_sum / number
    g_var = g_square / number - g_mean * g_mean
    c_mean = c_sum / number
    c_var = c_square / number - c_mean * c_mean
    factor = RESCALE * jnp.sqrt((c_var + 1.0) / (g_var + 1.0)) + (1.0 - RESCALE)
    vel = g_mean + (guided - g_mean) * factor
    keep = wide - 64
    out_ref[...] = jnp.where(cfg == 0, vel[:, :keep], vel[:, 64:]).astype(BF16)

    with scope("drain"):
        bytes_of(qhome.at[0:3], q_send)
        bytes_of(kvh.at[:, 0:7 * rows, :], kv_send)
        bytes_of(kvh.at[:, 0:8 * rows, :], kd_send)
        bytes_of(kvr.at[:, 0:7 * rows, :], ring_send)
        bytes_of(kvr.at[:, 0:8 * rows, :], d2d_send)
        bytes_of(oback, back_send)
        bytes_of(obuf.at[:, 0:nplane - 1], o_send)
        bytes_of(cbuf.at[0:nseq - 1, 0:1, :], cnt_send)
        bytes_of(statbuf.at[0:nseq - 1], st_send)
        bytes_of(wbuf.at[:, 0:(ntp - 1) * 64, :], w_send)
        bytes_of(wbuf.at[:, 0:(ntp - 1) * 64, :], wd_send)


def body(queries, keys, values, text_keys, text_values, prompt_lengths, frame_counts, out_weight):
    rows, width = queries.shape[1:]
    trows = text_keys.shape[1]
    heads = width // HD
    nseq, ntp = lax.axis_size("seq"), lax.axis_size("tp")
    model = out_weight.shape[1]
    cols = model // ntp
    keep = cols // 2
    wide = keep + 64
    vm = pl.BlockSpec(memory_space=pltpu.VMEM)
    sm = pl.BlockSpec(memory_space=pltpu.SMEM)
    hbm = pl.BlockSpec(memory_space=pl.ANY)
    dma = pltpu.SemaphoreType.DMA
    return pl.pallas_call(
        functools.partial(kernel, (heads, rows, trows, nseq, ntp, cols)),
        out_shape=jax.ShapeDtypeStruct((rows, keep), BF16),
        in_specs=[sm, sm, hbm, hbm, hbm, hbm, hbm, hbm],
        out_specs=vm,
        scratch_shapes=[
            pltpu.VMEM((rows, width), BF16),
            pltpu.VMEM((rows, width), BF16),
            pltpu.VMEM((trows, width), BF16),
            pltpu.VMEM((trows, width), BF16),
            pltpu.VMEM((8, HD), F32),
            pltpu.VMEM((3, rows, HD), BF16),
            pltpu.VMEM((3, 2, rows, HD), BF16),
            pltpu.VMEM((4, rows, HD), BF16),
            pltpu.VMEM((rows, HD), BF16),
            pltpu.VMEM((2, nseq * rows, HD), BF16),
            pltpu.VMEM((2, nseq * rows, HD), BF16),
            pltpu.VMEM((nseq * rows, HD), BF16),
            pltpu.VMEM((nseq * rows, HD), BF16),
            pltpu.VMEM((2, 2, trows, HD), BF16),
            pltpu.VMEM((trows, HD), BF16),
            pltpu.VMEM((nseq, 8, HD), F32),
            pltpu.VMEM((5, rows, HD), F32),
            pltpu.VMEM((5, rows, 2 * HD), F32),
            pltpu.VMEM((3, rows, HD), BF16),
            pltpu.VMEM((heads, 2 * ntp, rows, HD), BF16),
            pltpu.VMEM((heads, ntp * HD, wide), BF16),
            pltpu.VMEM((2, rows, wide), F32),
            pltpu.VMEM((16, HD), F32),
            pltpu.VMEM((nseq, 16, HD), F32),
            dma, dma((3,)), dma, dma((3,)), dma((4,)), dma, dma((4,)), dma((4,)),
            dma, dma((4, 4)), dma, dma((2, 8)), dma, dma, dma, dma((3,)),
            dma, dma((heads, 6)), dma, dma, dma, dma, dma, dma((9,)),
            dma, dma,
        ],
        compiler_params=pltpu.CompilerParams(
            collective_id=0, has_side_effects=True, vmem_limit_bytes=60 * 1024 * 1024
        ),
    )(
        prompt_lengths, frame_counts, queries[0], keys[0], values[0],
        text_keys[0], text_values[0], out_weight.reshape(heads, HD, model),
    )


def solution(mesh):
    placed = (
        P("cfg", "seq", "tp"),
        P("cfg", "seq", "tp"),
        P("cfg", "seq", "tp"),
        P("cfg", None, "tp"),
        P("cfg", None, "tp"),
        P("cfg"),
        P("seq"),
        P("tp", None),
    )
    return jax.shard_map(
        body, mesh=mesh, in_specs=placed, out_specs=P("seq", ("tp", "cfg")), check_vma=False
    )
```

time: 147 us -> 126 us (0.86)
  Pallas kernels: 144 us -> 122 us
    pallas_call x1, Pallas kernels: 144 us -> 122 us  [body(): pl.pallas_call(functools.partial(kernel, (heads, rows, trows, nseq, ntp,...]
where the time goes in v4:
time: 126 us
  Pallas kernels  122 us (97%)
  local copies, waits for them, and re-layouts  1.87 us (1%)
  between operations  1.3 us (1%)
    pallas_call x1, Pallas kernels, body(): pl.pallas_call(functools.partial(kernel, (heads, rows, trows, nseq, ntp,...  122 us

profile of v4, /device:TPU:1, one launch (start us, length us, event | category | flops | bytes accessed | tf_op | source)
XLA Modules:
  0.0 125.5 jit_solution(16321468498366237656)
XLA Ops:
  1.3 122.4 %shard_map.82 = bf16[480,320]{1,0:T(8,128)(2,1)} custom-call(s32[1]{0:T(128)S(6)} %copy.10.plen_ref, s32[1]{0:T(128)S(6)} %copy.11.count_ref, bf16[480,640]{1,0:T(8,128)(2,1)} %bitcast.9, bf16[480,640]{1,0:T(8,128)(2,1)} %bitcast.10, bf16[480,640]{1,0:T(8,128)(2,1)} %bitcast.11, bf16[512,640]{1,0:T(8,128)(2,1)} %bitcast.7, bf16[512,640]{1,0:T(8,128)(2,1)} %bitcast.8, ...), custom_call_target="tpu_custom_call" | custom-call | tf_op jit(solution)/shard_map/pallas_call | solution.py:595
  123.7 1.9 %copy.9 = bf16[480,320]{0,1:T(8,128)(2,1)} copy(bf16[480,320]{1,0:T(8,128)(2,1)} %shard_map.82) | data formatting | bytes 614400 | tf_op jit(solution)/shard_map/pallas_call | solution.py:595

commit v5 on v4

--- a/solution.py
+++ b/solution.py
@@ -85,6 +85,13 @@
     def bytes_of(ref, sem):
         pltpu.make_async_copy(ref, ref, sem).wait()
 
+    pairs = [(k_hbm, k_ref), (v_hbm, v_ref), (tk_hbm, tk_ref), (tv_hbm, tv_ref),
+             (q_hbm.at[:, lanes(head_of(0))], qhome.at[0]),
+             (q_hbm.at[:, lanes(heads - 1)], qring)]
+    pairs += [(q_hbm.at[:, lanes(head_of(u))], qout.at[u - 1]) for u in range(1, units)]
+    loads = [pltpu.make_async_copy(a, b, in_sem.at[i]) for i, (a, b) in enumerate(pairs)]
+    for copy in loads:
+        copy.start()
     barrier = pltpu.get_barrier_semaphore()
     for d in range(1, nseq):
         pl.semaphore_signal(barrier, inc=1, device_id={"seq": lax.rem(me + d, nseq)}, device_id_type=MESH)
@@ -92,20 +99,13 @@
         peer = lax.rem(spot + d, nplane)
         pl.semaphore_signal(barrier, inc=1, device_id={"cfg": peer // ntp, "tp": lax.rem(peer, ntp)},
                             device_id_type=MESH)
-    pairs = [(k_hbm, k_ref), (v_hbm, v_ref), (tk_hbm, tk_ref), (tv_hbm, tv_ref),
-             (q_hbm.at[:, lanes(head_of(0))], qhome.at[0]),
-             (q_hbm.at[:, lanes(heads - 1)], qring)]
-    pairs += [(q_hbm.at[:, lanes(head_of(u))], qout.at[u - 1]) for u in range(1, units)]
-    loads = [pltpu.make_async_copy(a, b, in_sem.at[i]) for i, (a, b) in enumerate(pairs)]
-    for copy in loads:
-        copy.start()
     cnt_in[...] = jnp.broadcast_to(count.astype(F32), cnt_in.shape)
     loads[0].wait()
     loads[1].wait()
 
     row_id = lax.broadcasted_iota(jnp.int32, (rows, HD), 0)
     trow_id = lax.broadcasted_iota(jnp.int32, (trows, HD), 0)
-    for u in range(units + 1):
+    def prepare(u):
         cut = lanes(head_of(u) if u < units else heads - 1)
         kk = k_ref[:, cut].astype(F32)
         vv = v_ref[:, cut].astype(F32)
@@ -120,6 +120,9 @@
         else:
             kvr[0, 0:rows, :] = kk
             kvr[1, 0:rows, :] = vv
+
+    for u in range(2):
+        prepare(u)
     for copy in loads[4:]:
         copy.wait()
 
@@ -232,7 +235,7 @@
             hand(u, 1, 0, -1, 0, 1, lower)
             for a in (-1, 1):
                 for d in (1, -1):
-                    hand(u, a, 0, 0, d, 3)
+                    hand(u, a, 0, 0, d, 3 if a < 0 else 6)
             blocks(u, 2, 2)
             hand(u, 0, -1, 0, 1, 5, upper)
             hand(u, 0, 1, 0, -1, 5, lower)
@@ -241,8 +244,8 @@
             for d in (1, -1):
                 hand(u, 2, 0, 0, d, 4)
         elif stage == 3:
-            blocks(u, 3, 4)
             for a in (-1, 1):
+                blocks(u, 3 if a < 0 else 6, 2)
                 hand(u, a, -1, 0, 1, 5, upper)
                 hand(u, a, 1, 0, -1, 5, lower)
             blocks(u, 4, 2)
@@ -257,8 +260,10 @@
     q_out(1).start()
     kv_out(1).start()
     kv_mate(0).start()
-    kv_out(2).start()
-    kv_out(3).start()
+    for u in range(2, units):
+        prepare(u)
+        kv_out(u).start()
+    prepare(units)
     own_w = pltpu.make_async_copy(
         w_hbm.at[:, :, window(tp)],
         wbuf.at[:, pl.ds(tp * HD, HD), :], w_loc)
@@ -424,25 +429,24 @@
             pass_on(0, 4)
             pass_on(3, 4)
 
-    order = [(0, 0), (1, 0), (0, 1), (1, 1), (0, 2), (1, 2), (0, 3), (1, 3),
+    order = [(0, 0), (1, 0), (0, 1), (1, 1), (0, 2), (0, 3), (1, 2), (1, 3),
              (2, 0), (2, 1), (2, 2), (2, 3), (3, 0), (3, 1), (3, 2), (3, 3)]
     ahead = {
         0: [lambda: arrive(1), lambda: ready(0)],
         1: [weights_out, lambda: wait_q(1), lambda: mark_home(1)],
         2: [lambda: arrive(2), lambda: arrive_buddy(1), lambda: arrive(3), lambda: ready(1)],
-        3: [lambda: mark_home(2)],
+        3: [lambda: mark_home(2), lambda: mark_home(3)],
         4: [lambda: arrive_buddy(2), q_out(2).start, lambda: ready(2)],
-        5: [lambda: mark_home(3)],
-        6: [lambda: arrive_buddy(3), q_out(3).start, lambda: ready(3)],
-        7: [lambda: to_obuf(0), lambda: relay(0, 0)],
+        5: [lambda: arrive_buddy(3), q_out(3).start, lambda: ready(3)],
+        6: [lambda: to_obuf(0), lambda: relay(0, 0)],
         8: [lambda: to_owner(1), launch, lambda: wait_q(2)],
         9: [lambda: relay(0, 1)],
         10: [lambda: relay(1, 0), weights_in],
         11: [lambda: relay(0, 2), lambda: hop(1, 0)],
         12: [lambda: to_owner(2), lambda: wait_q(3)],
-        13: [lambda: relay(0, 3), lambda: hop(1, 1)],
-        14: [lambda: relay(1, 1)],
-        15: [lambda: hop(2, 0)],
+        13: [lambda: relay(0, 3), lambda: relay(1, 1)],
+        14: [lambda: hop(1, 1)],
+        15: [lambda: relay(1, 2), lambda: hop(2, 0)],
     }
 
     def work(k, _):
@@ -465,17 +469,18 @@
     lax.fori_loop(0, len(order), work, 0)
     to_owner(3)
     relay(2, 0)
-    relay(1, 2)
     hop(2, 1)
     text(units)
-    hop(3, 0)
+    relay(1, 3)
     d2d(0, 0).wait_recv()
     d2d(1, 0).wait_recv()
     for sl in range(2):
         mark_ring(sl)
     stretch(0, 2)
-    relay(1, 3)
     relay(2, 1)
+    hop(3, 0)
+    relay(3, 0)
+    relay(2, 2)
     hop(3, 1)
 
     def far(s, _):
@@ -487,15 +492,14 @@
 
         @pl.when(s == 1)
         def _():
-            relay(3, 0)
+            relay(3, 1)
             d_in(2)
             for sl in range(6, 10):
                 mark_ring(sl)
 
         @pl.when(s == 2)
         def _():
-            x4()
-            relay(2, 2)
+            relay(2, 3)
             d_in(3)
             for sl in range(10, 16):
                 mark_ring(sl)
@@ -503,6 +507,7 @@
         return 0
 
     lax.fori_loop(0, 3, far, 0)
+    x4()
     with scope("ww2"):
         bytes_of(wbuf.at[:, 0:(ntp - 1) * 64, :], wd_recv)
         own_w.wait()
@@ -512,11 +517,9 @@
     relay(units, 0)
     relay(0, 4)
     project(0)
-    relay(3, 1)
-    relay(2, 3)
+    relay(3, 2)
     relay(1, 4)
     project(1)
-    relay(3, 2)
     relay(units, 1)
     relay(3, 3)
     relay(2, 4)
@@ -624,7 +627,7 @@
             pltpu.VMEM((nseq, 16, HD), F32),
             dma, dma((3,)), dma, dma((3,)), dma((4,)), dma, dma((4,)), dma((4,)),
             dma, dma((4, 4)), dma, dma((2, 8)), dma, dma, dma, dma((3,)),
-            dma, dma((heads, 6)), dma, dma, dma, dma, dma, dma((9,)),
+            dma, dma((heads, 7)), dma, dma, dma, dma, dma, dma((9,)),
             dma, dma,
         ],
         compiler_params=pltpu.CompilerParams(

time: 126 us -> 125 us (level)
  no operation moved by 1% of the time
where the time goes in v5:
time: 125 us
  Pallas kernels  122 us (98%)
  local copies, waits for them, and re-layouts  1.87 us (1%)
  between operations  1.3 us (1%)
    pallas_call x1, Pallas kernels, body(): pl.pallas_call(functools.partial(kernel, (heads, rows, trows, nseq, ntp,...  122 us

profile of v5, /device:TPU:1, one launch (start us, length us, event | category | flops | bytes accessed | tf_op | source)
XLA Modules:
  0.0 124.8 jit_solution(2402204873462587071)
XLA Ops:
  1.3 121.7 %shard_map.82 = bf16[480,320]{1,0:T(8,128)(2,1)} custom-call(s32[1]{0:T(128)S(6)} %copy.10.plen_ref, s32[1]{0:T(128)S(6)} %copy.11.count_ref, bf16[480,640]{1,0:T(8,128)(2,1)} %bitcast.9, bf16[480,640]{1,0:T(8,128)(2,1)} %bitcast.10, bf16[480,640]{1,0:T(8,128)(2,1)} %bitcast.11, bf16[512,640]{1,0:T(8,128)(2,1)} %bitcast.7, bf16[512,640]{1,0:T(8,128)(2,1)} %bitcast.8, ...), custom_call_target="tpu_custom_call" | custom-call | tf_op jit(solution)/shard_map/pallas_call | solution.py:598
  123.0 1.9 %copy.9 = bf16[480,320]{0,1:T(8,128)(2,1)} copy(bf16[480,320]{1,0:T(8,128)(2,1)} %shard_map.82) | data formatting | bytes 614400 | tf_op jit(solution)/shard_map/pallas_call | solution.py:598

commit v6 on v5

--- a/solution.py
+++ b/solution.py
@@ -424,21 +424,26 @@
         d2d(0, 0).start()
         d2d(1, 0).start()
 
+    def mark_all_ring():
+        for sl in range(nseq):
+            mark_ring(sl)
+
     def x4():
         with scope("x4"):
             pass_on(0, 4)
             pass_on(3, 4)
 
-    order = [(0, 0), (1, 0), (0, 1), (1, 1), (0, 2), (0, 3), (1, 2), (1, 3),
+    order = [(0, 0), (1, 0), (0, 1), (1, 1), (0, 2), (1, 2), (0, 3), (1, 3),
              (2, 0), (2, 1), (2, 2), (2, 3), (3, 0), (3, 1), (3, 2), (3, 3)]
     ahead = {
         0: [lambda: arrive(1), lambda: ready(0)],
         1: [weights_out, lambda: wait_q(1), lambda: mark_home(1)],
-        2: [lambda: arrive(2), lambda: arrive_buddy(1), lambda: arrive(3), lambda: ready(1)],
+        2: [lambda: arrive(2), mark_all_ring, lambda: arrive_buddy(1), lambda: arrive(3), lambda: ready(1)],
         3: [lambda: mark_home(2), lambda: mark_home(3)],
         4: [lambda: arrive_buddy(2), q_out(2).start, lambda: ready(2)],
-        5: [lambda: arrive_buddy(3), q_out(3).start, lambda: ready(3)],
-        6: [lambda: to_obuf(0), lambda: relay(0, 0)],
+        5: [lambda: arrive_buddy(3), q_out(3).start],
+        6: [lambda: ready(3)],
+        7: [lambda: to_obuf(0), lambda: relay(0, 0)],
         8: [lambda: to_owner(1), launch, lambda: wait_q(2)],
         9: [lambda: relay(0, 1)],
         10: [lambda: relay(1, 0), weights_in],
@@ -474,8 +479,6 @@
     relay(1, 3)
     d2d(0, 0).wait_recv()
     d2d(1, 0).wait_recv()
-    for sl in range(2):
-        mark_ring(sl)
     stretch(0, 2)
     relay(2, 1)
     hop(3, 0)
@@ -487,22 +490,16 @@
         @pl.when(s == 0)
         def _():
             d_in(1)
-            for sl in range(2, 6):
-                mark_ring(sl)
 
         @pl.when(s == 1)
         def _():
             relay(3, 1)
             d_in(2)
-            for sl in range(6, 10):
-                mark_ring(sl)
 
         @pl.when(s == 2)
         def _():
             relay(2, 3)
             d_in(3)
-            for sl in range(10, 16):
-                mark_ring(sl)
         stretch(2 + 4 * s, 4)
         return 0
 
@@ -543,17 +540,19 @@
     stat[...] = jnp.concatenate(lines + [jnp.zeros((16 - 4 * tiles, HD), F32)], axis=0)
     statbuf[me] = stat[...]
 
+    lead = 4 * tiles
+
     def st(d):
-        return remote(stat, statbuf.at[me], st_send, st_recv, seq=lax.rem(me + d, nseq))
+        return remote(stat.at[0:lead, :], statbuf.at[me, 0:lead, :], st_send, st_recv, seq=lax.rem(me + d, nseq))
 
     for d in range(1, nseq):
         st(d).start()
     with scope("stats"):
-        bytes_of(statbuf.at[0:nseq - 1], st_recv)
-    total = statbuf[0]
+        bytes_of(statbuf.at[0:nseq - 1, 0:lead, :], st_recv)
+    total = statbuf[0, 0:lead, :]
     number = cbuf[0][0:1, :]
     for i in range(1, nseq):
-        total = total + statbuf[i]
+        total = total + statbuf[i, 0:lead, :]
         number = number + cbuf[i][0:1, :]
     number = spread(number, wide)
     g_sum, g_square, c_sum, c_square = (
@@ -577,7 +576,7 @@
         bytes_of(oback, back_send)
         bytes_of(obuf.at[:, 0:nplane - 1], o_send)
         bytes_of(cbuf.at[0:nseq - 1, 0:1, :], cnt_send)
-        bytes_of(statbuf.at[0:nseq - 1], st_send)
+        bytes_of(statbuf.at[0:nseq - 1, 0:lead, :], st_send)
         bytes_of(wbuf.at[:, 0:(ntp - 1) * 64, :], w_send)
         bytes_of(wbuf.at[:, 0:(ntp - 1) * 64, :], wd_send)
 

time: 125 us -> 124 us (level)
  Pallas kernels: 122 us -> 120 us
    pallas_call x1, Pallas kernels: 122 us -> 120 us  [body(): pl.pallas_call(functools.partial(kernel, (heads, rows, trows, nseq, ntp,...]
where the time goes in v6:
time: 124 us; the launch traced here: 123 us
  Pallas kernels  120 us (97%)
  local copies, waits for them, and re-layouts  1.87 us (2%)
  between operations  1.3 us (1%)
    pallas_call x1, Pallas kernels, body(): pl.pallas_call(functools.partial(kernel, (heads, rows, trows, nseq, ntp,...  120 us

profile of v6, /device:TPU:1, one launch (start us, length us, event | category | flops | bytes accessed | tf_op | source)
XLA Modules:
  0.0 123.5 jit_solution(16520768213489615998)
XLA Ops:
  1.3 120.3 %shard_map.82 = bf16[480,320]{1,0:T(8,128)(2,1)} custom-call(s32[1]{0:T(128)S(6)} %copy.10.plen_ref, s32[1]{0:T(128)S(6)} %copy.11.count_ref, bf16[480,640]{1,0:T(8,128)(2,1)} %bitcast.9, bf16[480,640]{1,0:T(8,128)(2,1)} %bitcast.10, bf16[480,640]{1,0:T(8,128)(2,1)} %bitcast.11, bf16[512,640]{1,0:T(8,128)(2,1)} %bitcast.7, bf16[512,640]{1,0:T(8,128)(2,1)} %bitcast.8, ...), custom_call_target="tpu_custom_call" | custom-call | tf_op jit(solution)/shard_map/pallas_call | solution.py:597
  121.6 1.9 %copy.9 = bf16[480,320]{0,1:T(8,128)(2,1)} copy(bf16[480,320]{1,0:T(8,128)(2,1)} %shard_map.82) | data formatting | bytes 614400 | tf_op jit(solution)/shard_map/pallas_call | solution.py:597
